TPU v7x, 32 devices: a whole 2x2x4 slice. The times are simulated.
32 devices in a mesh: pix: 8 (over z, x), frm: 4 (over y, core).
Axes of the slice: x: 2, y: 2, z: 4, core: 2. Of those that a mesh axis runs over, the one named last changes fastest.
Arguments:
- frames_y: bfloat16 [1024, 2048], P('pix', 'frm'), may hold values from -6 to 6
- traces: bfloat16 [1024, 2048], P('pix', 'frm'), may hold values from -0.13183594 to 0.13183594
- footprints: float32 [1024, 1024], P('pix'), may hold values from 0 to 2
- order: int32 [1024], replicated, may hold values from 0 to 1023, each once
- support: int32 [8, 256], P('pix'), may hold values from 0 to 1023, as said below
Outputs:
- footprints_new: float32 [1024, 1024], P('pix')
Inputs may be any that keep to these rules, and one draw needn't show every extreme that they name: `support`: row j lists 256 different neurons; it governs pixels j * 128 to (j + 1) * 128 - 1.
All inputs are finite; a program needn't handle non-finite values.
Results may differ from a plain program's by a relative error of at most 0.0003.
Values may be sent and summed in bfloat16 or wider, within the bound.
No kernel may reach another device: no remote copies, remote signals or barrier semaphores. Data moves between devices by JAX's collectives and lax.ppermute only.
A program may use at most 64 MiB of HBM per device.

v0:
```python
import functools

import jax
import jax.numpy as jnp
from jax import lax
from jax.experimental import pallas as pl
from jax.experimental.pallas import tpu as pltpu
from jax.sharding import PartitionSpec as P


BLK = 128
SWEEPS = 3
LANES = 128
EXTRA = 8
CHUNK = 512


VMEM_BYTES = 60 * 1024 * 1024


def spread(frames_y, traces, footprints, order, support):
    highest = lax.Precision.HIGHEST
    pix_rows = frames_y.shape[0]
    neurons = footprints.shape[1]
    total_pixels = pix_rows * lax.axis_size("pix")
    contract = (((1,), (1,)), ((), ()))
    stacked = jnp.concatenate([frames_y, traces], axis=0)
    terms = lax.dot_general(
        stacked,
        lax.all_gather(traces, "pix", axis=0, tiled=True),
        contract,
        preferred_element_type=jnp.float32,
    )
    cross, gram_part = lax.psum((terms[:pix_rows], terms[pix_rows:]), "frm")
    gram = lax.all_gather(gram_part, "pix", axis=0, tiled=True)
    neuron_ids = lax.iota(jnp.int32, neurons)
    member = jnp.any(support[0][:, None] == neuron_ids[None, :], axis=0).astype(jnp.float32)
    keep_perm = jnp.take(member, order)
    current = jnp.take(footprints, order, axis=1)
    cross_perm = jnp.take(cross, order, axis=1)
    gram_perm = jnp.take(jnp.take(gram, order, axis=0), order, axis=1)
    diagonal = jnp.diagonal(gram_perm)
    block_count = neurons // BLK
    for _ in range(SWEEPS):
        for block_index in range(block_count):
            lower = block_index * BLK
            upper = lower + BLK
            numer = cross_perm[:, lower:upper] - jnp.dot(
                current, gram_perm[:, lower:upper], precision=highest
            )
            update = keep_perm[lower:upper] * jnp.maximum(
                current[:, lower:upper] + numer / diagonal[lower:upper], 0.0
            )
            squares = lax.psum(jnp.sum(update * update, axis=0), "pix")
            scale = jnp.sqrt(squares / total_pixels + 1e-06)
            current = current.at[:, lower:upper].set(update / scale)
    return jnp.zeros_like(current).at[:, order].set(current)


f32 = jnp.float32
bf16 = jnp.bfloat16


def dot(a, b):
    return jnp.dot(a, b, preferred_element_type=f32)


def dot_t(a, b):
    return lax.dot_general(a, b, (((1,), (1,)), ((), ())), preferred_element_type=f32)


def split2(x):
    hi = x.astype(bf16)
    return hi, (x - hi.astype(f32)).astype(bf16)


def split3(x):
    hi = x.astype(bf16)
    rest = x - hi.astype(f32)
    mid = rest.astype(bf16)
    return hi, mid, (rest - mid.astype(f32)).astype(bf16)


def join3(x):
    rows = x.shape[0] // 3
    return x[:rows] + x[rows : 2 * rows] + x[2 * rows :]


def as_column(row_ref):
    return jnp.broadcast_to(row_ref[...], (LANES, row_ref.shape[1])).T


def one_hot_into(out_ref, column, row_ref):
    for lower in range(0, row_ref.shape[1], LANES):
        hit = column == row_ref[:, lower : lower + LANES]
        out_ref[:, lower : lower + LANES] = jnp.where(hit, 1.0, 0.0).astype(bf16)


def setup_kernel(order_ref, ids_ref, support_ref, foot_ref, frames_ref, traces_ref, *outs):
    column_ref, perm, members, foot_hl, listed, frames_out, traces_out = outs
    frames_out[...] = frames_ref[...]
    traces_out[...] = traces_ref[...]
    pixels = foot_ref.shape[0]
    width = support_ref.shape[1]
    column = as_column(order_ref)
    column_ref[...] = column
    one_hot_into(perm, column, ids_ref)
    one_hot_into(members, column, support_ref)
    foot = join3(dot_t(jnp.concatenate(split3(foot_ref[...]), axis=0), perm[...]))
    hi, lo = split2(foot)
    foot_hl[:pixels, :] = hi
    foot_hl[pixels:, :] = lo
    ids = jnp.broadcast_to(support_ref[...].astype(f32), (EXTRA, width))
    listed[...] = jnp.concatenate([ids, ids], axis=1)


def gram_kernel(m, held, rows, perm, members, foot_hl, listed, *refs):
    y_refs, refs = refs[:m], refs[m:]
    t_refs, refs = refs[: len(held)], refs[len(held) :]
    g_ref, own_ref, mine_ref = refs[:3]
    t_all, y_all, t_perm, gram, split = refs[3:]
    neurons = perm.shape[0]
    pixels, frames = y_refs[0].shape
    me, here = lax.axis_index("frm"), lax.axis_index("pix")
    for g in range(m):
        y_all[me ^ g] = y_refs[g][...]
    for names, ref in zip(held, t_refs):
        for place, (s, g) in enumerate(names):
            to = pl.ds(pl.multiple_of((here ^ s) * rows, rows), rows)
            t_all[me ^ g, to, :] = ref[place * rows : (place + 1) * rows, :]
    for f in range(m):
        for lower in range(0, neurons, 256):
            part = dot(perm[lower : lower + 256, :], t_all[f])
            t_perm[lower : lower + 256, f * frames : (f + 1) * frames] = part.astype(bf16)
    for lower in range(0, neurons, 256):
        gram[lower : lower + 256, :] = dot_t(t_perm[lower : lower + 256, :], t_perm[...])
    cross = jnp.zeros((pixels, neurons), f32)
    for f in range(m):
        cross += dot_t(y_all[f], t_perm[:, f * frames : (f + 1) * frames])
    eye = lax.broadcasted_iota(jnp.int32, (BLK, BLK), 0) == lax.broadcasted_iota(
        jnp.int32, (BLK, BLK), 1
    )
    for lower in range(0, neurons, BLK):
        upper = lower + BLK
        square = gram[lower:upper, lower:upper]
        inverse = 1.0 / jnp.sum(jnp.where(eye, square, 0.0), axis=0, keepdims=True)
        gram[lower:upper, lower:upper] = jnp.where(eye, 0.0, square)
        hi, lo = split2(gram[:, lower:upper] * inverse)
        g_ref[:, 2 * lower : 2 * lower + BLK] = hi
        g_ref[:, 2 * lower + BLK : 2 * upper] = lo
        right = cross[:, lower:upper] * inverse
        both = dot(foot_hl[:, lower:], g_ref[lower:, 2 * lower : 2 * upper])
        both = both[:pixels] + both[pixels:]
        first = right - (both[:, :BLK] + both[:, BLK:])
        for index, part in enumerate(split3(first)):
            split[index * 2 * pixels : index * 2 * pixels + pixels, lower:upper] = part
        for index, part in enumerate(split3(right)):
            split[index * 2 * pixels + pixels : (index + 1) * 2 * pixels, lower:upper] = part
    packed = join3(dot(split[...], members[...]))
    width = members.shape[1]
    own_ref[:, :width] = packed[:pixels]
    own_ref[:, width:] = packed[pixels:]
    half = pixels // 2
    mine_ref[:half, :] = own_ref[pl.ds((me % 2) * half, half), :]
    mine_ref[half:, :] = listed[...]


def sweep_kernel(n, column_ref, perm, mine_members, own_ref, g_ref, *refs):
    mine_refs, refs = refs[: n - 1], refs[n - 1 :]
    other_refs, refs = refs[: n - 1], refs[n - 1 :]
    out_ref = refs[0]
    members, packed, keep, first, right, weights, cur, ahead, fresh, result = refs[1:]
    neurons = perm.shape[0]
    pixels, width2 = own_ref.shape
    width = width2 // 2
    half = pixels // 2
    blocks = neurons // BLK
    mine = lax.axis_index("frm") % 2
    column = column_ref[...]
    for block in range(blocks):
        piece = g_ref[block * BLK : (block + 1) * BLK, :]
        weights[2 * block * BLK : (2 * block + 1) * BLK, :] = piece
        weights[(2 * block + 1) * BLK : 2 * (block + 1) * BLK, :] = piece
    ones = jnp.ones((16, width), bf16)
    for s in range(n):
        if s == 0:
            packed[...] = own_ref[...]
            members[...] = mine_members[...]
        else:
            packed[pl.ds(mine * half, half), :] = mine_refs[s - 1][:half, :]
            packed[pl.ds((1 - mine) * half, half), :] = other_refs[s - 1][:half, :]
            listed = mine_refs[s - 1][half : half + 1, :width].astype(jnp.int32)
            one_hot_into(members, column, listed)
        stacked = jnp.concatenate(
            [part for x in (packed[:, :width], packed[:, width:]) for part in split3(x)] + [ones],
            axis=0,
        )
        wide = dot_t(stacked, members[...])
        rows = slice(s * pixels, (s + 1) * pixels)
        first[rows, :] = join3(wide[: 3 * pixels])
        right[rows, :] = join3(wide[3 * pixels : 6 * pixels])
        keep[s : s + 1, :] = wide[6 * pixels : 6 * pixels + 1]
    total = n * pixels

    def tile(block):
        return slice(2 * block * BLK, 2 * (block + 1) * BLK)

    def look_ahead(block, spans, slot):
        for start in range(0, total, CHUNK):
            rows = slice(start, start + CHUNK)
            terms = [
                dot(cur[rows, 2 * lower * BLK : 2 * upper * BLK],
                    weights[2 * lower * BLK : 2 * upper * BLK, tile(block)])
                for lower, upper in spans if upper > lower
            ]
            if terms:
                both = sum(terms[1:], terms[0])
                ahead[slot, rows, :] = both[:, :BLK] + both[:, BLK:]

    def step(block, previous, has_ahead, source, next_block, next_spans):
        lower, upper = block * BLK, (block + 1) * BLK
        squares = jnp.zeros((8, BLK), f32)
        if previous is not None:
            for start in range(0, total, CHUNK):
                rows = slice(start, start + CHUNK)
                both = dot(cur[rows, tile(previous)], weights[tile(previous), tile(block)])
                fresh[rows, :] = both[:, :BLK] + both[:, BLK:]
        for s in range(n):
            rows = slice(s * pixels, (s + 1) * pixels)
            value = source[rows, lower:upper]
            if has_ahead:
                value = value - ahead[block % 2, rows, :]
            if previous is not None:
                value = value - fresh[rows, :]
            value = keep[s : s + 1, lower:upper] * jnp.maximum(value, 0.0)
            fresh[rows, :] = value
            squares += jnp.sum((value * value).reshape(pixels // 8, 8, BLK), axis=0)
        if next_block is not None:
            look_ahead(next_block, next_spans, next_block % 2)
        mean = jnp.sum(squares, axis=0, keepdims=True) / total
        inverse = 1.0 / jnp.sqrt(mean + 1e-06)
        for s in range(n):
            rows = slice(s * pixels, (s + 1) * pixels)
            value = fresh[rows, :] * inverse
            if s == 0:
                result[:, lower:upper] = value
            hi, lo = split2(value)
            cur[rows, 2 * lower : 2 * lower + BLK] = hi
            cur[rows, 2 * lower + BLK : 2 * upper] = lo

    last = blocks - 1
    for block in range(blocks):
        previous = block - 1 if block else None
        if block < last:
            step(block, previous, block > 1, first, block + 1, [(0, block)])
        else:
            step(block, previous, block > 1, first, 0, [(0, last)])

    @pl.loop(0, SWEEPS - 1)
    def _(_):
        for block in range(blocks):
            after = (block + 1) % blocks
            spans = [(0, block), (block + 1, blocks)]
            step(block, (block - 1) % blocks, True, right, after, spans)

    out_ref[...] = join3(dot(jnp.concatenate(split3(result[...]), axis=0), perm[...]))


def replicated(n, m, frames_y, traces, footprints, order, support):
    pixels, frames = frames_y.shape
    rows = traces.shape[0]
    neurons = footprints.shape[1]
    width = support.shape[1]

    def swap(x, dp, df):
        pairs = [(p * m + f, (p ^ dp) * m + (f ^ df)) for p in range(n) for f in range(m)]
        return lax.ppermute(x, ("pix", "frm"), pairs)

    def stack(xs):
        return jnp.concatenate(xs, axis=0) if len(xs) > 1 else xs[0]

    shape = jax.ShapeDtypeStruct
    vmem = pl.BlockSpec(memory_space=pltpu.VMEM)
    total = n * pixels

    def call(kernel, flops, outs, scratch, limit, *args):
        moving = sum(x.size * x.dtype.itemsize for x in args)
        return pl.pallas_call(
            kernel,
            out_shape=outs,
            in_specs=[vmem] * len(args),
            out_specs=jax.tree.map(lambda _: vmem, outs),
            scratch_shapes=[pltpu.VMEM(*x) for x in scratch],
            compiler_params=pltpu.CompilerParams(vmem_limit_bytes=limit * VMEM_BYTES // 60),
            cost_estimate=pl.CostEstimate(flops=flops, bytes_accessed=moving, transcendentals=0),
        )(*args)

    order_row = order.reshape(1, neurons)
    natural = lax.iota(jnp.int32, neurons).reshape(1, neurons)
    bits = [1 << k for k in range(n.bit_length() - 2, 0, -1)]
    far = {0: traces}
    for bit in bits:
        far[bit] = swap(traces, bit, 0)
    blobs, y = [], {0: frames_y}

    def beside(names, blob):
        blobs.append(([(s, g ^ 1) for s, g in names], swap(blob, 0, 1)))

    def named(group, ds, dg):
        return [(s ^ ds, dg) for s in group]

    def spread_near(group, blob, way):
        along = swap(blob, 1, 0)
        near, relays = [(named(group, 1, 0), along)], []
        for g in range(2, m, 2):
            across = swap(blob, 0, g)
            near.append((named(group, 0, g), across))
            if way == "direct":
                near.append((named(group, 1, g), swap(blob, 1, g)))
            else:
                hop = (across, 1, 0) if way == "x" else (along, 0, g)
                relays.append((named(group, 1, g), hop))
        return near, relays

    own_near, own_relays = spread_near([0], traces, "y")
    for g in range(2, m, 2):
        y[g] = swap(frames_y, 0, g)
    singles = []
    for bit in bits[1:]:
        for s in [s for s in far if s & -s > bit]:
            far[s ^ bit] = swap(far[s], bit, 0)
            singles.append(s ^ bit)
    pair, relays = [], []
    if bits:
        pair_blob = stack([far[bit] for bit in bits])
        pair, relays = spread_near(bits, pair_blob, "x")
    own_near += [(names, swap(*hop)) for names, hop in own_relays]
    beside([(0, 0)], traces)
    for g in range(0, m, 2):
        y[g + 1] = swap(y[g], 0, 1)
    if bits:
        beside(named(bits, 0, 0), pair_blob)
        blobs.append((named(bits, 0, 0), pair_blob))
    later = []
    for s in singles:
        near, _ = spread_near([s], far[s], "direct")
        later += near
        beside([(s, 0)], far[s])
        blobs.append(([(s, 0)], far[s]))
    pair += [(names, swap(*hop)) for names, hop in relays]
    column, perm, members, foot_hl, listed, own_frames, traces_here = call(
        setup_kernel,
        6 * pixels * neurons * neurons,
        (
            shape((neurons, LANES), jnp.int32),
            shape((neurons, neurons), bf16),
            shape((neurons, width), bf16),
            shape((2 * pixels, neurons), bf16),
            shape((EXTRA, 2 * width), f32),
            shape((pixels, frames), bf16),
            shape((rows, frames), bf16),
        ),
        [],
        16,
        order_row, natural, support, footprints, frames_y, traces,
    )
    for entry in own_near + pair + later:
        beside(*entry)
    blobs += [([(0, 0)], traces_here)] + own_near + pair + later

    g, own, mine = call(
        functools.partial(gram_kernel, m, [names for names, _ in blobs], rows),
        4 * neurons * neurons * m * frames,
        (
            shape((neurons, 2 * neurons), bf16),
            shape((pixels, 2 * width), f32),
            shape((pixels // 2 + EXTRA, 2 * width), f32),
        ),
        [
            ((m, neurons, frames), bf16),
            ((m, pixels, frames), bf16),
            ((neurons, m * frames), bf16),
            ((neurons, neurons), f32),
            ((6 * pixels, neurons), bf16),
        ],
        36,
        perm, members, foot_hl, listed,
        own_frames,
        *[y[k] for k in range(1, m)],
        *[blob for _, blob in blobs],
    )
    got = {0: mine}
    for bit in bits:
        got[bit] = swap(mine, bit, 0)
    got[1] = swap(mine, 1, 0)
    others = {}
    for bit in bits[::-1]:
        got[bit ^ 1] = swap(got[bit], 1, 0)
        if bit != bits[0]:
            for s in [s for s in list(got) if s & -s > bit]:
                got[s ^ bit] = swap(got[s], bit, 0)
    for s in list(got):
        if s and s ^ 1 not in got:
            got[s ^ 1] = swap(got[s], 1, 0)
    for s in got:
        if s:
            others[s] = swap(got[s], 0, 1)
    mines = [got[s] for s in range(1, n)]
    others = [others[s] for s in range(1, n)]
    return call(
        functools.partial(sweep_kernel, n),
        2 * SWEEPS * 4 * total * neurons * neurons,
        shape((pixels, neurons), f32),
        [
            ((neurons, width), bf16),
            ((pixels, 2 * width), f32),
            ((n, neurons), f32),
            ((total, neurons), f32),
            ((total, neurons), f32),
            ((2 * neurons, 2 * neurons), bf16),
            ((total, 2 * neurons), bf16),
            ((2, total, BLK), f32),
            ((total, BLK), f32),
            ((pixels, neurons), f32),
        ],
        40,
        column, perm, members, own, g, *mines, *others,
    )


def power_of_two(x):
    return x > 1 and x & (x - 1) == 0


def solution(mesh):
    n, m = mesh.shape["pix"], mesh.shape["frm"]

    def local(frames_y, traces, footprints, order, support):
        neurons = footprints.shape[1]
        total = n * frames_y.shape[0]
        fits = 12 * total * neurons + 10 * neurons * neurons <= VMEM_BYTES // 2
        lined = neurons % 256 == 0 and traces.shape[0] % LANES == 0
        if fits and lined and power_of_two(n) and power_of_two(m):
            return replicated(n, m, frames_y, traces, footprints, order, support)
        return spread(frames_y, traces, footprints, order, support)

    in_specs = (P("pix", "frm"), P("pix", "frm"), P("pix", None), P(), P("pix", None))
    out_specs = P("pix", None)
    return jax.shard_map(local, mesh=mesh, in_specs=in_specs, out_specs=out_specs, check_vma=False)
```

profile of v0, /device:TPU:0, one launch (start us, length us, event | category | flops | bytes accessed | tf_op | source)
XLA Modules:
  0.0 120.4 jit_solution(5543411913613773)
XLA Ops:
  0.0 4.1 %collective-permute-start.4 = (bf16[128,512]{1,0:T(8,128)(2,1)}, bf16[128,512]{1,0:T(8,128)(2,1)S(1)}, u32[]{:S(2)}, u32[]{:S(2)}) collective-permute-start(bf16[128,512]{1,0:T(8,128)(2,1)} %traces_ref.1), channel_id=1, source_target_pairs={{0,16},{1,17},{2,18},{3,19},{4,20},{5,21},{6,22},{7,23},{8,24},{9,... | collective-permute-start | bytes 393224 | tf_op jit(solution)/shard_map/ppermute | solution.py:277
  4.1 1.5 %collective-permute-start.1 = (bf16[128,512]{1,0:T(8,128)(2,1)}, bf16[128,512]{1,0:T(8,128)(2,1)S(1)}, u32[]{:S(2)}, u32[]{:S(2)}) collective-permute-start(bf16[128,512]{1,0:T(8,128)(2,1)} %frames_ref.1), channel_id=1, source_target_pairs={{0,2},{1,3},{2,0},{3,1},{4,6},{5,7},{6,4},{7,5},{8,10},{9,11},{10,... | collective-permute-start | bytes 393224 | tf_op jit(solution)/shard_map/ppermute | solution.py:277
  5.6 1.6 %collective-permute-start.5 = (bf16[128,512]{1,0:T(8,128)(2,1)}, bf16[128,512]{1,0:T(8,128)(2,1)S(1)}, u32[]{:S(2)}, u32[]{:S(2)}) collective-permute-start(bf16[128,512]{1,0:T(8,128)(2,1)} %traces_ref.1), channel_id=1, source_target_pairs={{0,8},{1,9},{2,10},{3,11},{4,12},{5,13},{6,14},{7,15},{8,0},{9,1},... | collective-permute-start | bytes 393224 | tf_op jit(solution)/shard_map/ppermute | solution.py:277
  7.2 0.5 collective-permute-start.3
  7.7 3.0 %collective-permute-done.4 = bf16[128,512]{1,0:T(8,128)(2,1)S(1)} collective-permute-done((bf16[128,512]{1,0:T(8,128)(2,1)}, bf16[128,512]{1,0:T(8,128)(2,1)S(1)}, u32[]{:S(2)}, u32[]{:S(2)}) %collective-permute-start.4) | collective-permute-done | bytes 131104 | tf_op jit(solution)/shard_map/ppermute | solution.py:277
  10.7 1.6 %collective-permute-start.11 = (bf16[128,512]{1,0:T(8,128)(2,1)}, bf16[128,512]{1,0:T(8,128)(2,1)S(1)}, u32[]{:S(2)}, u32[]{:S(2)}) collective-permute-start(bf16[128,512]{1,0:T(8,128)(2,1)} %traces_ref.1), channel_id=1, source_target_pairs={{0,2},{1,3},{2,0},{3,1},{4,6},{5,7},{6,4},{7,5},{8,10},{9,11},{10,... | collective-permute-start | bytes 393224 | tf_op jit(solution)/shard_map/ppermute | solution.py:277
  12.3 0.0 collective-permute-done.1.refs_2_
  12.3 1.6 %collective-permute-start.9 = (bf16[128,512]{1,0:T(8,128)(2,1)}, bf16[128,512]{1,0:T(8,128)(2,1)S(1)}, u32[]{:S(2)}, u32[]{:S(2)}) collective-permute-start(bf16[128,512]{1,0:T(8,128)(2,1)} %traces_ref.1), channel_id=1, source_target_pairs={{0,4},{1,5},{2,6},{3,7},{4,0},{5,1},{6,2},{7,3},{8,12},{9,13},{10,... | collective-permute-start | bytes 393224 | tf_op jit(solution)/shard_map/ppermute | solution.py:277
  13.9 0.0 collective-permute-done.refs_1_
  13.9 0.6 collective-permute-start.17
  14.4 0.7 collective-permute-start.7
  15.2 0.7 collective-permute-done.11.refs_20_
  15.9 1.7 %collective-permute-done.9.refs_19_ = bf16[128,512]{1,0:T(8,128)(2,1)S(1)} collective-permute-done((bf16[128,512]{1,0:T(8,128)(2,1)}, bf16[128,512]{1,0:T(8,128)(2,1)S(1)}, u32[]{:S(2)}, u32[]{:S(2)}) %collective-permute-start.9) | collective-permute-done | bytes 131104 | tf_op jit(solution)/shard_map/ppermute | solution.py:277
  17.5 0.5 collective-permute-start.13
  18.0 2.1 %collective-permute-done.7.refs_8_ = bf16[128,512]{1,0:T(8,128)(2,1)S(1)} collective-permute-done((bf16[128,512]{1,0:T(8,128)(2,1)S(1)}, bf16[128,512]{1,0:T(8,128)(2,1)S(1)}, u32[]{:S(2)}, u32[]{:S(2)}) %collective-permute-start.7) | collective-permute-done | bytes 131104 | tf_op jit(solution)/shard_map/ppermute | solution.py:277
  20.1 1.5 %collective-permute-start.25 = (bf16[128,512]{1,0:T(8,128)(2,1)S(1)}, bf16[128,512]{1,0:T(8,128)(2,1)S(1)}, u32[]{:S(2)}, u32[]{:S(2)}) collective-permute-start(bf16[128,512]{1,0:T(8,128)(2,1)S(1)} %collective-permute-done.7.refs_8_), channel_id=1, source_target_pairs={{0,6},{1,7},{2,4},{3,5},{4,2},{5,3},{6,0},{7,1},{8,14},{9,15},{10,... | collective-permute-start | bytes 393224 | tf_op jit(solution)/shard_map/ppermute | solution.py:277
  21.6 0.5 collective-permute-start.23
  22.0 6.7 %collective-permute-done.13.refs_21_ = bf16[128,512]{1,0:T(8,128)(2,1)S(1)} collective-permute-done((bf16[128,512]{1,0:T(8,128)(2,1)S(1)}, bf16[128,512]{1,0:T(8,128)(2,1)S(1)}, u32[]{:S(2)}, u32[]{:S(2)}) %collective-permute-start.13) | collective-permute-done | bytes 131104 | tf_op jit(solution)/shard_map/ppermute | solution.py:277
  28.7 0.5 collective-permute-start.21
  29.3 0.0 collective-permute-done.10.refs_9_
  29.3 1.5 %collective-permute-start.15 = (bf16[256,512]{1,0:T(8,128)(2,1)S(1)}, bf16[256,512]{1,0:T(8,128)(2,1)S(1)}, u32[]{:S(2)}, u32[]{:S(2)}) collective-permute-start(bf16[256,512]{1,0:T(8,128)(2,1)S(1)} %constant_dynamic-update-slice_fusion.refs_6_), channel_id=1, source_target_pairs={{0,4},{1,5},{2,6},{3,7},{4,0},{5,1},{6,2},{7,3},{8,12},{9,13},{10,... | collective-permute-start | bytes 786440 | tf_op jit(solution)/shard_map/ppermute | solution.py:277
  30.8 0.5 collective-permute-start.19
  31.3 0.0 collective-permute-done.25.refs_27_
  31.3 0.5 collective-permute-start.8
  31.8 3.3 %collective-permute-done.21.refs_25_ = bf16[128,512]{1,0:T(8,128)(2,1)S(1)} collective-permute-done((bf16[128,512]{1,0:T(8,128)(2,1)S(1)}, bf16[128,512]{1,0:T(8,128)(2,1)S(1)}, u32[]{:S(2)}, u32[]{:S(2)}) %collective-permute-start.21) | collective-permute-done | bytes 131104 | tf_op jit(solution)/shard_map/ppermute | solution.py:277
  35.1 0.5 collective-permute-start.18
  35.6 0.8 collective-permute-done.14.refs_11_
  36.4 0.1 collective-permute-start.26
  36.6 4.1 %collective-permute-done.15.refs_22_ = bf16[256,512]{1,0:T(8,128)(2,1)S(1)} collective-permute-done((bf16[256,512]{1,0:T(8,128)(2,1)S(1)}, bf16[256,512]{1,0:T(8,128)(2,1)S(1)}, u32[]{:S(2)}, u32[]{:S(2)}) %collective-permute-start.15) | collective-permute-done | bytes 262176 | tf_op jit(solution)/shard_map/ppermute | solution.py:277
  40.7 0.0 collective-permute-start.16
  40.7 3.8 %collective-permute-done.19.refs_24_ = bf16[256,512]{1,0:T(8,128)(2,1)S(1)} collective-permute-done((bf16[256,512]{1,0:T(8,128)(2,1)S(1)}, bf16[256,512]{1,0:T(8,128)(2,1)S(1)}, u32[]{:S(2)}, u32[]{:S(2)}) %collective-permute-start.19) | collective-permute-done | bytes 262176 | tf_op jit(solution)/shard_map/ppermute | solution.py:277
  44.6 0.0 collective-permute-start.20
  44.6 0.0 collective-permute-done.6.refs_5_
  44.6 0.5 collective-permute-start.24
  45.1 0.0 collective-permute-done.26.refs_17_
  45.1 0.1 collective-permute-start.22
  45.1 1.0 copy-done
  46.2 0.9 copy-done.1
  47.1 0.9 copy-done.2
  48.0 0.7 copy-done.3
  48.7 0.7 copy-done.4
  49.4 1.5 %shard_map.55 = (s32[1024,128]{1,0:T(8,128)S(1)}, bf16[1024,1024]{1,0:T(8,128)(2,1)S(1)}, bf16[1024,256]{1,0:T(8,128)(2,1)S(1)}, bf16[256,1024]{1,0:T(8,128)(2,1...) custom-call(s32[1,1024]{1,0:T(1,128)S(1)} %bitcast.1, ...), custom_call_target="tpu_custom_call" | custom-call | flops 805306368 | bytes 795648 | tf_op jit(solution)/shard_map/pallas_call | solution.py:288
  50.8 0.0 collective-permute-done.24.refs_16_
  50.9 0.0 collective-permute-done.18.refs_13_
  50.9 0.0 collective-permute-done.16.refs_12_
  50.9 12.7 %shard_map.56 = (bf16[1024,2048]{1,0:T(8,128)(2,1)S(1)}, f32[128,512]{1,0:T(8,128)S(1)}, f32[72,512]{1,0:T(8,128)S(1)}) custom-call(bf16[1024,1024]{1,0:T(8,128)(2,1)S(1)} %get-tuple-element.16.perm, bf16[1024,256]{1,0:T(8,128)(2,1)S(1)} %get-tuple-element.17.members.mine_members, bf16[256,1024]{1,0:T(8,128)(2,1)S(1)} %get-tuple-element.18.foot_hl, ...), custom_call_target="tpu_custom_call" | custom-call | flops 8589934592 | bytes 7880704 | tf_op jit(solution)/shard_map/pallas_call | solution.py:288
  63.6 0.9 collective-permute-start.30
  64.5 3.1 %collective-permute-start.28 = (f32[72,512]{1,0:T(8,128)S(1)}, f32[72,512]{1,0:T(8,128)S(1)}, u32[]{:S(2)}, u32[]{:S(2)}) collective-permute-start(f32[72,512]{1,0:T(8,128)S(1)} %get-tuple-element.24), channel_id=1, source_target_pairs={{0,8},{1,9},{2,10},{3,11},{4,12},{5,13},{6,14},{7,15},{8,0},{9,1},... | collective-permute-start | bytes 442376 | tf_op jit(solution)/shard_map/ppermute | solution.py:277
  67.6 1.0 collective-permute-start.27
  68.6 5.4 %collective-permute-done.30.refs_3_ = f32[72,512]{1,0:T(8,128)S(1)} collective-permute-done((f32[72,512]{1,0:T(8,128)S(1)}, f32[72,512]{1,0:T(8,128)S(1)}, u32[]{:S(2)}, u32[]{:S(2)}) %collective-permute-start.30) | collective-permute-done | bytes 147488 | tf_op jit(solution)/shard_map/ppermute | solution.py:277
  74.0 0.0 collective-permute-start.32
  74.0 0.5 collective-permute-start.31
  74.6 0.0 collective-permute-done.28.refs_1_
  74.6 0.2 collective-permute-start.35
  74.8 1.5 %collective-permute-start.29 = (f32[72,512]{1,0:T(8,128)S(1)}, f32[72,512]{1,0:T(8,128)S(1)}, u32[]{:S(2)}, u32[]{:S(2)}) collective-permute-start(f32[72,512]{1,0:T(8,128)S(1)} %collective-permute-done.28.refs_1_), channel_id=1, source_target_pairs={{0,4},{1,5},{2,6},{3,7},{4,0},{5,1},{6,2},{7,3},{8,12},{9,13},{10,... | collective-permute-start | bytes 442376 | tf_op jit(solution)/shard_map/ppermute | solution.py:277
  76.3 3.0 %collective-permute-done.32.refs_5_ = f32[72,512]{1,0:T(8,128)S(1)} collective-permute-done((f32[72,512]{1,0:T(8,128)S(1)}, f32[72,512]{1,0:T(8,128)S(1)}, u32[]{:S(2)}, u32[]{:S(2)}) %collective-permute-start.32) | collective-permute-done | bytes 147488 | tf_op jit(solution)/shard_map/ppermute | solution.py:277
  79.3 0.5 collective-permute-start.33
  79.8 0.9 collective-permute-done.31.refs_4_
  80.8 0.0 collective-permute-start.39
  80.8 0.5 collective-permute-start.38
  81.3 2.6 %collective-permute-done.29.refs_2_ = f32[72,512]{1,0:T(8,128)S(1)} collective-permute-done((f32[72,512]{1,0:T(8,128)S(1)}, f32[72,512]{1,0:T(8,128)S(1)}, u32[]{:S(2)}, u32[]{:S(2)}) %collective-permute-start.29) | collective-permute-done | bytes 147488 | tf_op jit(solution)/shard_map/ppermute | solution.py:277
  83.9 2.7 %collective-permute-done.33.refs_6_ = f32[72,512]{1,0:T(8,128)S(1)} collective-permute-done((f32[72,512]{1,0:T(8,128)S(1)}, f32[72,512]{1,0:T(8,128)S(1)}, u32[]{:S(2)}, u32[]{:S(2)}) %collective-permute-start.33) | collective-permute-done | bytes 147488 | tf_op jit(solution)/shard_map/ppermute | solution.py:277
  86.6 1.3 %collective-permute-done.40.refs_13_ = f32[72,512]{1,0:T(8,128)S(1)} collective-permute-done((f32[72,512]{1,0:T(8,128)S(1)}, f32[72,512]{1,0:T(8,128)S(1)}, u32[]{:S(2)}, u32[]{:S(2)}) %collective-permute-start.40) | collective-permute-done | bytes 147488 | tf_op jit(solution)/shard_map/ppermute | solution.py:277
  88.0 32.4 %shard_map.57 = f32[128,1024]{1,0:T(8,128)} custom-call(s32[1024,128]{1,0:T(8,128)S(1)} %get-tuple-element.15.column_ref, bf16[1024,1024]{1,0:T(8,128)(2,1)S(1)} %get-tuple-element.16.perm, bf16[1024,256]{1,0:T(8,128)(2,1)S(1)} %get-tuple-element.17.members.mine_members, f32[128,512]{1,0:T(8,128)S(1)} %get-tuple-element.22.own_ref, ...), custom_call_target="tpu_custom_call" | custom-call | flops 25769803776 | bytes 9666560 | tf_op jit(solution)/shard_map/pallas_call | solution.py:288
  (34 shorter events, 0.1 us)
Async XLA Ops:
  0.0 10.7 %collective-permute-start.4 = (bf16[128,512]{1,0:T(8,128)(2,1)}, bf16[128,512]{1,0:T(8,128)(2,1)S(1)}, u32[]{:S(2)}, u32[]{:S(2)}) collective-permute-start(bf16[128,512]{1,0:T(8,128)(2,1)} %traces_ref.1), channel_id=1, source_target_pairs={{0,16},{1,17},{2,18},{3,19},{4,20},{5,21},{6,22},{7,23},{8,24},{9,... | collective-permute-start | bytes 393224 | tf_op jit(solution)/shard_map/ppermute | solution.py:277
  4.1 8.2 %collective-permute-start.1 = (bf16[128,512]{1,0:T(8,128)(2,1)}, bf16[128,512]{1,0:T(8,128)(2,1)S(1)}, u32[]{:S(2)}, u32[]{:S(2)}) collective-permute-start(bf16[128,512]{1,0:T(8,128)(2,1)} %frames_ref.1), channel_id=1, source_target_pairs={{0,2},{1,3},{2,0},{3,1},{4,6},{5,7},{6,4},{7,5},{8,10},{9,11},{10,... | collective-permute-start | bytes 393224 | tf_op jit(solution)/shard_map/ppermute | solution.py:277
  5.6 8.2 %collective-permute-start.5 = (bf16[128,512]{1,0:T(8,128)(2,1)}, bf16[128,512]{1,0:T(8,128)(2,1)S(1)}, u32[]{:S(2)}, u32[]{:S(2)}) collective-permute-start(bf16[128,512]{1,0:T(8,128)(2,1)} %traces_ref.1), channel_id=1, source_target_pairs={{0,8},{1,9},{2,10},{3,11},{4,12},{5,13},{6,14},{7,15},{8,0},{9,1},... | collective-permute-start | bytes 393224 | tf_op jit(solution)/shard_map/ppermute | solution.py:277
  7.2 6.7 %collective-permute-start = (bf16[128,512]{1,0:T(8,128)(2,1)}, bf16[128,512]{1,0:T(8,128)(2,1)S(1)}, u32[]{:S(2)}, u32[]{:S(2)}) collective-permute-start(bf16[128,512]{1,0:T(8,128)(2,1)} %frames_ref.1), channel_id=1, source_target_pairs={{0,1},{1,0},{2,3},{3,2},{4,5},{5,4},{6,7},{7,6},{8,9},{9,8},{10,11... | collective-permute-start | bytes 393224 | tf_op jit(solution)/shard_map/ppermute | solution.py:277
  7.2 7.3 %collective-permute-start.3 = (bf16[128,512]{1,0:T(8,128)(2,1)}, bf16[128,512]{1,0:T(8,128)(2,1)S(1)}, u32[]{:S(2)}, u32[]{:S(2)}) collective-permute-start(bf16[128,512]{1,0:T(8,128)(2,1)} %traces_ref.1), channel_id=1, source_target_pairs={{0,1},{1,0},{2,3},{3,2},{4,5},{5,4},{6,7},{7,6},{8,9},{9,8},{10,11... | collective-permute-start | bytes 393224 | tf_op jit(solution)/shard_map/ppermute | solution.py:277
  10.7 5.2 %collective-permute-start.11 = (bf16[128,512]{1,0:T(8,128)(2,1)}, bf16[128,512]{1,0:T(8,128)(2,1)S(1)}, u32[]{:S(2)}, u32[]{:S(2)}) collective-permute-start(bf16[128,512]{1,0:T(8,128)(2,1)} %traces_ref.1), channel_id=1, source_target_pairs={{0,2},{1,3},{2,0},{3,1},{4,6},{5,7},{6,4},{7,5},{8,10},{9,11},{10,... | collective-permute-start | bytes 393224 | tf_op jit(solution)/shard_map/ppermute | solution.py:277
  12.3 5.2 %collective-permute-start.9 = (bf16[128,512]{1,0:T(8,128)(2,1)}, bf16[128,512]{1,0:T(8,128)(2,1)S(1)}, u32[]{:S(2)}, u32[]{:S(2)}) collective-permute-start(bf16[128,512]{1,0:T(8,128)(2,1)} %traces_ref.1), channel_id=1, source_target_pairs={{0,4},{1,5},{2,6},{3,7},{4,0},{5,1},{6,2},{7,3},{8,12},{9,13},{10,... | collective-permute-start | bytes 393224 | tf_op jit(solution)/shard_map/ppermute | solution.py:277
  13.8 4.1 %collective-permute-start.2 = (bf16[128,512]{1,0:T(8,128)(2,1)S(1)}, bf16[128,512]{1,0:T(8,128)(2,1)S(1)}, u32[]{:S(2)}, u32[]{:S(2)}) collective-permute-start(bf16[128,512]{1,0:T(8,128)(2,1)S(1)} %collective-permute-done.1.refs_2_), channel_id=1, source_target_pairs={{0,1},{1,0},{2,3},{3,2},{4,5},{5,4},{6,7},{7,6},{8,9},{9,8},{10,11... | collective-permute-start | bytes 393224 | tf_op jit(solution)/shard_map/ppermute | solution.py:277
  13.9 16.9 %collective-permute-start.17 = (bf16[256,512]{1,0:T(8,128)(2,1)S(1)}, bf16[256,512]{1,0:T(8,128)(2,1)S(1)}, u32[]{:S(2)}, u32[]{:S(2)}) collective-permute-start(bf16[256,512]{1,0:T(8,128)(2,1)S(1)} %constant_dynamic-update-slice_fusion.refs_6_), channel_id=1, source_target_pairs={{0,2},{1,3},{2,0},{3,1},{4,6},{5,7},{6,4},{7,5},{8,10},{9,11},{10,... | collective-permute-start | bytes 786440 | tf_op jit(solution)/shard_map/ppermute | solution.py:277
  14.4 5.6 %collective-permute-start.7 = (bf16[128,512]{1,0:T(8,128)(2,1)S(1)}, bf16[128,512]{1,0:T(8,128)(2,1)S(1)}, u32[]{:S(2)}, u32[]{:S(2)}) collective-permute-start(bf16[128,512]{1,0:T(8,128)(2,1)S(1)} %collective-permute-done.4), channel_id=1, source_target_pairs={{0,8},{1,9},{2,10},{3,11},{4,12},{5,13},{6,14},{7,15},{8,0},{9,1},... | collective-permute-start | bytes 393224 | tf_op jit(solution)/shard_map/ppermute | solution.py:277
  15.9 5.7 %collective-permute-start.12 = (bf16[128,512]{1,0:T(8,128)(2,1)S(1)}, bf16[128,512]{1,0:T(8,128)(2,1)S(1)}, u32[]{:S(2)}, u32[]{:S(2)}) collective-permute-start(bf16[128,512]{1,0:T(8,128)(2,1)S(1)} %collective-permute-done.11.refs_20_), channel_id=1, source_target_pairs={{0,1},{1,0},{2,3},{3,2},{4,5},{5,4},{6,7},{7,6},{8,9},{9,8},{10,11... | collective-permute-start | bytes 393224 | tf_op jit(solution)/shard_map/ppermute | solution.py:277
  17.5 11.2 %collective-permute-start.13 = (bf16[128,512]{1,0:T(8,128)(2,1)S(1)}, bf16[128,512]{1,0:T(8,128)(2,1)S(1)}, u32[]{:S(2)}, u32[]{:S(2)}) collective-permute-start(bf16[128,512]{1,0:T(8,128)(2,1)S(1)} %collective-permute-done.9.refs_19_), channel_id=1, source_target_pairs={{0,2},{1,3},{2,0},{3,1},{4,6},{5,7},{6,4},{7,5},{8,10},{9,11},{10,... | collective-permute-start | bytes 393224 | tf_op jit(solution)/shard_map/ppermute | solution.py:277
  18.0 11.3 %collective-permute-start.10 = (bf16[128,512]{1,0:T(8,128)(2,1)S(1)}, bf16[128,512]{1,0:T(8,128)(2,1)S(1)}, u32[]{:S(2)}, u32[]{:S(2)}) collective-permute-start(bf16[128,512]{1,0:T(8,128)(2,1)S(1)} %collective-permute-done.9.refs_19_), channel_id=1, source_target_pairs={{0,1},{1,0},{2,3},{3,2},{4,5},{5,4},{6,7},{7,6},{8,9},{9,8},{10,11... | collective-permute-start | bytes 393224 | tf_op jit(solution)/shard_map/ppermute | solution.py:277
  20.1 11.2 %collective-permute-start.25 = (bf16[128,512]{1,0:T(8,128)(2,1)S(1)}, bf16[128,512]{1,0:T(8,128)(2,1)S(1)}, u32[]{:S(2)}, u32[]{:S(2)}) collective-permute-start(bf16[128,512]{1,0:T(8,128)(2,1)S(1)} %collective-permute-done.7.refs_8_), channel_id=1, source_target_pairs={{0,6},{1,7},{2,4},{3,5},{4,2},{5,3},{6,0},{7,1},{8,14},{9,15},{10,... | collective-permute-start | bytes 393224 | tf_op jit(solution)/shard_map/ppermute | solution.py:277
  21.6 9.7 %collective-permute-start.23 = (bf16[128,512]{1,0:T(8,128)(2,1)S(1)}, bf16[128,512]{1,0:T(8,128)(2,1)S(1)}, u32[]{:S(2)}, u32[]{:S(2)}) collective-permute-start(bf16[128,512]{1,0:T(8,128)(2,1)S(1)} %collective-permute-done.7.refs_8_), channel_id=1, source_target_pairs={{0,2},{1,3},{2,0},{3,1},{4,6},{5,7},{6,4},{7,5},{8,10},{9,11},{10,... | collective-permute-start | bytes 393224 | tf_op jit(solution)/shard_map/ppermute | solution.py:277
  28.7 6.4 %collective-permute-start.21 = (bf16[128,512]{1,0:T(8,128)(2,1)S(1)}, bf16[128,512]{1,0:T(8,128)(2,1)S(1)}, u32[]{:S(2)}, u32[]{:S(2)}) collective-permute-start(bf16[128,512]{1,0:T(8,128)(2,1)S(1)} %collective-permute-done.7.refs_8_), channel_id=1, source_target_pairs={{0,4},{1,5},{2,6},{3,7},{4,0},{5,1},{6,2},{7,3},{8,12},{9,13},{10,... | collective-permute-start | bytes 393224 | tf_op jit(solution)/shard_map/ppermute | solution.py:277
  29.3 11.4 %collective-permute-start.15 = (bf16[256,512]{1,0:T(8,128)(2,1)S(1)}, bf16[256,512]{1,0:T(8,128)(2,1)S(1)}, u32[]{:S(2)}, u32[]{:S(2)}) collective-permute-start(bf16[256,512]{1,0:T(8,128)(2,1)S(1)} %constant_dynamic-update-slice_fusion.refs_6_), channel_id=1, source_target_pairs={{0,4},{1,5},{2,6},{3,7},{4,0},{5,1},{6,2},{7,3},{8,12},{9,13},{10,... | collective-permute-start | bytes 786440 | tf_op jit(solution)/shard_map/ppermute | solution.py:277
  30.8 13.8 %collective-permute-start.19 = (bf16[256,512]{1,0:T(8,128)(2,1)S(1)}, bf16[256,512]{1,0:T(8,128)(2,1)S(1)}, u32[]{:S(2)}, u32[]{:S(2)}) collective-permute-start(bf16[256,512]{1,0:T(8,128)(2,1)S(1)} %collective-permute-done.17.refs_23_), channel_id=1, source_target_pairs={{0,4},{1,5},{2,6},{3,7},{4,0},{5,1},{6,2},{7,3},{8,12},{9,13},{10,... | collective-permute-start | bytes 786440 | tf_op jit(solution)/shard_map/ppermute | solution.py:277
  31.3 13.3 %collective-permute-start.6 = (bf16[256,512]{1,0:T(8,128)(2,1)S(1)}, bf16[256,512]{1,0:T(8,128)(2,1)S(1)}, u32[]{:S(2)}, u32[]{:S(2)}) collective-permute-start(bf16[256,512]{1,0:T(8,128)(2,1)S(1)} %constant_dynamic-update-slice_fusion.refs_6_), channel_id=1, source_target_pairs={{0,1},{1,0},{2,3},{3,2},{4,5},{5,4},{6,7},{7,6},{8,9},{9,8},{10,11... | collective-permute-start | bytes 786440 | tf_op jit(solution)/shard_map/ppermute | solution.py:277
  31.3 3.8 %collective-permute-start.8 = (bf16[128,512]{1,0:T(8,128)(2,1)S(1)}, bf16[128,512]{1,0:T(8,128)(2,1)S(1)}, u32[]{:S(2)}, u32[]{:S(2)}) collective-permute-start(bf16[128,512]{1,0:T(8,128)(2,1)S(1)} %collective-permute-done.7.refs_8_), channel_id=1, source_target_pairs={{0,1},{1,0},{2,3},{3,2},{4,5},{5,4},{6,7},{7,6},{8,9},{9,8},{10,11... | collective-permute-start | bytes 393224 | tf_op jit(solution)/shard_map/ppermute | solution.py:277
  35.1 1.3 %collective-permute-start.14 = (bf16[128,512]{1,0:T(8,128)(2,1)S(1)}, bf16[128,512]{1,0:T(8,128)(2,1)S(1)}, u32[]{:S(2)}, u32[]{:S(2)}) collective-permute-start(bf16[128,512]{1,0:T(8,128)(2,1)S(1)} %collective-permute-done.13.refs_21_), channel_id=1, source_target_pairs={{0,1},{1,0},{2,3},{3,2},{4,5},{5,4},{6,7},{7,6},{8,9},{9,8},{10,11... | collective-permute-start | bytes 393224 | tf_op jit(solution)/shard_map/ppermute | solution.py:277
  35.1 15.8 %collective-permute-start.18 = (bf16[256,512]{1,0:T(8,128)(2,1)S(1)}, bf16[256,512]{1,0:T(8,128)(2,1)S(1)}, u32[]{:S(2)}, u32[]{:S(2)}) collective-permute-start(bf16[256,512]{1,0:T(8,128)(2,1)S(1)} %collective-permute-done.17.refs_23_), channel_id=1, source_target_pairs={{0,1},{1,0},{2,3},{3,2},{4,5},{5,4},{6,7},{7,6},{8,9},{9,8},{10,11... | collective-permute-start | bytes 786440 | tf_op jit(solution)/shard_map/ppermute | solution.py:277
  36.4 8.6 %collective-permute-start.26 = (bf16[128,512]{1,0:T(8,128)(2,1)S(1)}, bf16[128,512]{1,0:T(8,128)(2,1)S(1)}, u32[]{:S(2)}, u32[]{:S(2)}) collective-permute-start(bf16[128,512]{1,0:T(8,128)(2,1)S(1)} %collective-permute-done.25.refs_27_), channel_id=1, source_target_pairs={{0,1},{1,0},{2,3},{3,2},{4,5},{5,4},{6,7},{7,6},{8,9},{9,8},{10,11... | collective-permute-start | bytes 393224 | tf_op jit(solution)/shard_map/ppermute | solution.py:277
  40.7 10.2 %collective-permute-start.16 = (bf16[256,512]{1,0:T(8,128)(2,1)S(1)}, bf16[256,512]{1,0:T(8,128)(2,1)S(1)}, u32[]{:S(2)}, u32[]{:S(2)}) collective-permute-start(bf16[256,512]{1,0:T(8,128)(2,1)S(1)} %collective-permute-done.15.refs_22_), channel_id=1, source_target_pairs={{0,1},{1,0},{2,3},{3,2},{4,5},{5,4},{6,7},{7,6},{8,9},{9,8},{10,11... | collective-permute-start | bytes 786440 | tf_op jit(solution)/shard_map/ppermute | solution.py:277
  44.6 6.3 %collective-permute-start.20 = (bf16[256,512]{1,0:T(8,128)(2,1)S(1)}, bf16[256,512]{1,0:T(8,128)(2,1)S(1)}, u32[]{:S(2)}, u32[]{:S(2)}) collective-permute-start(bf16[256,512]{1,0:T(8,128)(2,1)S(1)} %collective-permute-done.19.refs_24_), channel_id=1, source_target_pairs={{0,1},{1,0},{2,3},{3,2},{4,5},{5,4},{6,7},{7,6},{8,9},{9,8},{10,11... | collective-permute-start | bytes 786440 | tf_op jit(solution)/shard_map/ppermute | solution.py:277
  44.6 6.3 %collective-permute-start.24 = (bf16[128,512]{1,0:T(8,128)(2,1)S(1)}, bf16[128,512]{1,0:T(8,128)(2,1)S(1)}, u32[]{:S(2)}, u32[]{:S(2)}) collective-permute-start(bf16[128,512]{1,0:T(8,128)(2,1)S(1)} %collective-permute-done.23.refs_26_), channel_id=1, source_target_pairs={{0,1},{1,0},{2,3},{3,2},{4,5},{5,4},{6,7},{7,6},{8,9},{9,8},{10,11... | collective-permute-start | bytes 393224 | tf_op jit(solution)/shard_map/ppermute | solution.py:277
  45.1 5.8 %collective-permute-start.22 = (bf16[128,512]{1,0:T(8,128)(2,1)S(1)}, bf16[128,512]{1,0:T(8,128)(2,1)S(1)}, u32[]{:S(2)}, u32[]{:S(2)}) collective-permute-start(bf16[128,512]{1,0:T(8,128)(2,1)S(1)} %collective-permute-done.21.refs_25_), channel_id=1, source_target_pairs={{0,1},{1,0},{2,3},{3,2},{4,5},{5,4},{6,7},{7,6},{8,9},{9,8},{10,11... | collective-permute-start | bytes 393224 | tf_op jit(solution)/shard_map/ppermute | solution.py:277
  45.1 1.0 copy-start
  46.2 0.9 copy-start.1
  47.1 0.9 copy-start.2
  48.0 0.7 copy-start.3
  48.7 0.7 copy-start.4
  63.6 10.4 %collective-permute-start.30 = (f32[72,512]{1,0:T(8,128)S(1)}, f32[72,512]{1,0:T(8,128)S(1)}, u32[]{:S(2)}, u32[]{:S(2)}) collective-permute-start(f32[72,512]{1,0:T(8,128)S(1)} %get-tuple-element.24), channel_id=1, source_target_pairs={{0,16},{1,17},{2,18},{3,19},{4,20},{5,21},{6,22},{7,23},{8,24},{9,... | collective-permute-start | bytes 442376 | tf_op jit(solution)/shard_map/ppermute | solution.py:277
  64.5 10.1 %collective-permute-start.28 = (f32[72,512]{1,0:T(8,128)S(1)}, f32[72,512]{1,0:T(8,128)S(1)}, u32[]{:S(2)}, u32[]{:S(2)}) collective-permute-start(f32[72,512]{1,0:T(8,128)S(1)} %get-tuple-element.24), channel_id=1, source_target_pairs={{0,8},{1,9},{2,10},{3,11},{4,12},{5,13},{6,14},{7,15},{8,0},{9,1},... | collective-permute-start | bytes 442376 | tf_op jit(solution)/shard_map/ppermute | solution.py:277
  67.6 7.2 %collective-permute-start.27 = (f32[72,512]{1,0:T(8,128)S(1)}, f32[72,512]{1,0:T(8,128)S(1)}, u32[]{:S(2)}, u32[]{:S(2)}) collective-permute-start(f32[72,512]{1,0:T(8,128)S(1)} %get-tuple-element.24), channel_id=1, source_target_pairs={{0,4},{1,5},{2,6},{3,7},{4,0},{5,1},{6,2},{7,3},{8,12},{9,13},{10,... | collective-permute-start | bytes 442376 | tf_op jit(solution)/shard_map/ppermute | solution.py:277
  74.0 5.3 %collective-permute-start.32 = (f32[72,512]{1,0:T(8,128)S(1)}, f32[72,512]{1,0:T(8,128)S(1)}, u32[]{:S(2)}, u32[]{:S(2)}) collective-permute-start(f32[72,512]{1,0:T(8,128)S(1)} %collective-permute-done.30.refs_3_), channel_id=1, source_target_pairs={{0,8},{1,9},{2,10},{3,11},{4,12},{5,13},{6,14},{7,15},{8,0},{9,1},... | collective-permute-start | bytes 442376 | tf_op jit(solution)/shard_map/ppermute | solution.py:277
  74.0 5.8 %collective-permute-start.37 = (f32[72,512]{1,0:T(8,128)S(1)}, f32[72,512]{1,0:T(8,128)S(1)}, u32[]{:S(2)}, u32[]{:S(2)}) collective-permute-start(f32[72,512]{1,0:T(8,128)S(1)} %collective-permute-done.30.refs_3_), channel_id=1, source_target_pairs={{0,1},{1,0},{2,3},{3,2},{4,5},{5,4},{6,7},{7,6},{8,9},{9,8},{10,11... | collective-permute-start | bytes 442376 | tf_op jit(solution)/shard_map/ppermute | solution.py:277
  74.0 6.7 %collective-permute-start.31 = (f32[72,512]{1,0:T(8,128)S(1)}, f32[72,512]{1,0:T(8,128)S(1)}, u32[]{:S(2)}, u32[]{:S(2)}) collective-permute-start(f32[72,512]{1,0:T(8,128)S(1)} %collective-permute-done.30.refs_3_), channel_id=1, source_target_pairs={{0,4},{1,5},{2,6},{3,7},{4,0},{5,1},{6,2},{7,3},{8,12},{9,13},{10,... | collective-permute-start | bytes 442376 | tf_op jit(solution)/shard_map/ppermute | solution.py:277
  74.6 6.2 %collective-permute-start.35 = (f32[72,512]{1,0:T(8,128)S(1)}, f32[72,512]{1,0:T(8,128)S(1)}, u32[]{:S(2)}, u32[]{:S(2)}) collective-permute-start(f32[72,512]{1,0:T(8,128)S(1)} %collective-permute-done.28.refs_1_), channel_id=1, source_target_pairs={{0,1},{1,0},{2,3},{3,2},{4,5},{5,4},{6,7},{7,6},{8,9},{9,8},{10,11... | collective-permute-start | bytes 442376 | tf_op jit(solution)/shard_map/ppermute | solution.py:277
  74.8 9.1 %collective-permute-start.29 = (f32[72,512]{1,0:T(8,128)S(1)}, f32[72,512]{1,0:T(8,128)S(1)}, u32[]{:S(2)}, u32[]{:S(2)}) collective-permute-start(f32[72,512]{1,0:T(8,128)S(1)} %collective-permute-done.28.refs_1_), channel_id=1, source_target_pairs={{0,4},{1,5},{2,6},{3,7},{4,0},{5,1},{6,2},{7,3},{8,12},{9,13},{10,... | collective-permute-start | bytes 442376 | tf_op jit(solution)/shard_map/ppermute | solution.py:277
  79.3 7.3 %collective-permute-start.33 = (f32[72,512]{1,0:T(8,128)S(1)}, f32[72,512]{1,0:T(8,128)S(1)}, u32[]{:S(2)}, u32[]{:S(2)}) collective-permute-start(f32[72,512]{1,0:T(8,128)S(1)} %collective-permute-done.32.refs_5_), channel_id=1, source_target_pairs={{0,4},{1,5},{2,6},{3,7},{4,0},{5,1},{6,2},{7,3},{8,12},{9,13},{10,... | collective-permute-start | bytes 442376 | tf_op jit(solution)/shard_map/ppermute | solution.py:277
  79.8 6.8 %collective-permute-start.34 = (f32[72,512]{1,0:T(8,128)S(1)}, f32[72,512]{1,0:T(8,128)S(1)}, u32[]{:S(2)}, u32[]{:S(2)}) collective-permute-start(f32[72,512]{1,0:T(8,128)S(1)} %collective-permute-done.27.refs_0_), channel_id=1, source_target_pairs={{0,1},{1,0},{2,3},{3,2},{4,5},{5,4},{6,7},{7,6},{8,9},{9,8},{10,11... | collective-permute-start | bytes 442376 | tf_op jit(solution)/shard_map/ppermute | solution.py:277
  80.8 5.9 %collective-permute-start.39 = (f32[72,512]{1,0:T(8,128)S(1)}, f32[72,512]{1,0:T(8,128)S(1)}, u32[]{:S(2)}, u32[]{:S(2)}) collective-permute-start(f32[72,512]{1,0:T(8,128)S(1)} %collective-permute-done.32.refs_5_), channel_id=1, source_target_pairs={{0,1},{1,0},{2,3},{3,2},{4,5},{5,4},{6,7},{7,6},{8,9},{9,8},{10,11... | collective-permute-start | bytes 442376 | tf_op jit(solution)/shard_map/ppermute | solution.py:277
  80.8 5.9 %collective-permute-start.38 = (f32[72,512]{1,0:T(8,128)S(1)}, f32[72,512]{1,0:T(8,128)S(1)}, u32[]{:S(2)}, u32[]{:S(2)}) collective-permute-start(f32[72,512]{1,0:T(8,128)S(1)} %collective-permute-done.31.refs_4_), channel_id=1, source_target_pairs={{0,1},{1,0},{2,3},{3,2},{4,5},{5,4},{6,7},{7,6},{8,9},{9,8},{10,11... | collective-permute-start | bytes 442376 | tf_op jit(solution)/shard_map/ppermute | solution.py:277
  83.9 2.7 %collective-permute-start.36 = (f32[72,512]{1,0:T(8,128)S(1)}, f32[72,512]{1,0:T(8,128)S(1)}, u32[]{:S(2)}, u32[]{:S(2)}) collective-permute-start(f32[72,512]{1,0:T(8,128)S(1)} %collective-permute-done.29.refs_2_), channel_id=1, source_target_pairs={{0,1},{1,0},{2,3},{3,2},{4,5},{5,4},{6,7},{7,6},{8,9},{9,8},{10,11... | collective-permute-start | bytes 442376 | tf_op jit(solution)/shard_map/ppermute | solution.py:277
  86.6 1.4 %collective-permute-start.40 = (f32[72,512]{1,0:T(8,128)S(1)}, f32[72,512]{1,0:T(8,128)S(1)}, u32[]{:S(2)}, u32[]{:S(2)}) collective-permute-start(f32[72,512]{1,0:T(8,128)S(1)} %collective-permute-done.33.refs_6_), channel_id=1, source_target_pairs={{0,1},{1,0},{2,3},{3,2},{4,5},{5,4},{6,7},{7,6},{8,9},{9,8},{10,11... | collective-permute-start | bytes 442376 | tf_op jit(solution)/shard_map/ppermute | solution.py:277
where the time goes:
time: 121 us; the launch traced here: 120 us
  Pallas kernels  46.6 us (39%)
  waiting for transfers between devices  42.3 us (35%)
  starting transfers between devices  27.1 us (22%)
  local copies, waits for them, and re-layouts  4.24 us (4%)
    pallas_call x3, Pallas kernels, call(): pl.pallas_call(kernel, out_shape=outs, in_specs=[vmem] * len(args), out_s...  46.6 us
    ppermute x41, waiting for transfers between devices, swap(): return lax.ppermute(x, ('pix', 'frm'), pairs)  42.3 us
    ppermute x41, starting transfers between devices, swap(): return lax.ppermute(x, ('pix', 'frm'), pairs)  27.1 us
    unnamed x11, local copies, waits for them, and re-layouts  4.22 us
  transfers between devices with their start and end apart: 41, of which 15 were waited for; matrix products, arithmetic and copies ran while one was open for 0% of the time, Pallas kernels for 1%

commit v1 on v0

--- a/solution.py
+++ b/solution.py
@@ -13,6 +13,8 @@
 LANES = 128
 EXTRA = 8
 CHUNK = 512
+UNPACK_MIB = 16
+SWEEP_MIB = 16
 
 
 VMEM_BYTES = 60 * 1024 * 1024
@@ -165,41 +167,53 @@
     mine_ref[half:, :] = listed[...]
 
 
-def sweep_kernel(n, column_ref, perm, mine_members, own_ref, g_ref, *refs):
-    mine_refs, refs = refs[: n - 1], refs[n - 1 :]
-    other_refs, refs = refs[: n - 1], refs[n - 1 :]
-    out_ref = refs[0]
-    members, packed, keep, first, right, weights, cur, ahead, fresh, result = refs[1:]
-    neurons = perm.shape[0]
-    pixels, width2 = own_ref.shape
-    width = width2 // 2
-    half = pixels // 2
-    blocks = neurons // BLK
+def unpack_kernel(blocks_at, mine_at, *refs):
+    column_ref, refs = refs[0], refs[1:]
+    inputs, outs = refs[: mine_at], refs[mine_at:]
+    first, right, keep = outs[:3]
+    members, packed = outs[-2:]
+    column = column_ref[...]
+    pixels, width2 = packed.shape
+    width, half = width2 // 2, pixels // 2
     mine = lax.axis_index("frm") % 2
-    column = column_ref[...]
-    for block in range(blocks):
-        piece = g_ref[block * BLK : (block + 1) * BLK, :]
-        weights[2 * block * BLK : (2 * block + 1) * BLK, :] = piece
-        weights[(2 * block + 1) * BLK : 2 * (block + 1) * BLK, :] = piece
     ones = jnp.ones((16, width), bf16)
-    for s in range(n):
-        if s == 0:
-            packed[...] = own_ref[...]
-            members[...] = mine_members[...]
+    at = 0
+    for place, own in enumerate(blocks_at):
+        if own:
+            packed[...] = inputs[at][...]
+            members[...] = inputs[at + 1][...]
+            g_ref, weights = inputs[at + 2], outs[3]
+            for lower in range(0, g_ref.shape[0], BLK):
+                piece = g_ref[lower : lower + BLK, :]
+                weights[2 * lower : 2 * lower + BLK, :] = piece
+                weights[2 * lower + BLK : 2 * (lower + BLK), :] = piece
+            at += 3
         else:
-            packed[pl.ds(mine * half, half), :] = mine_refs[s - 1][:half, :]
-            packed[pl.ds((1 - mine) * half, half), :] = other_refs[s - 1][:half, :]
-            listed = mine_refs[s - 1][half : half + 1, :width].astype(jnp.int32)
+            packed[pl.ds(mine * half, half), :] = inputs[at][:half, :]
+            packed[pl.ds((1 - mine) * half, half), :] = inputs[at + 1][:half, :]
+            listed = inputs[at][half : half + 1, :width].astype(jnp.int32)
             one_hot_into(members, column, listed)
+            at += 2
         stacked = jnp.concatenate(
             [part for x in (packed[:, :width], packed[:, width:]) for part in split3(x)] + [ones],
             axis=0,
         )
         wide = dot_t(stacked, members[...])
-        rows = slice(s * pixels, (s + 1) * pixels)
+        rows = slice(place * pixels, (place + 1) * pixels)
         first[rows, :] = join3(wide[: 3 * pixels])
         right[rows, :] = join3(wide[3 * pixels : 6 * pixels])
-        keep[s : s + 1, :] = wide[6 * pixels : 6 * pixels + 1]
+        keep[8 * place : 8 * place + 8, :] = wide[6 * pixels : 6 * pixels + 8]
+
+
+def sweep_kernel(sizes, perm, weights, *refs):
+    parts = len(sizes)
+    firsts, rights, keeps = refs[:parts], refs[parts : 2 * parts], refs[2 * parts : 3 * parts]
+    out_ref, cur, ahead, fresh, result = refs[3 * parts :]
+    neurons = perm.shape[0]
+    pixels = result.shape[0]
+    blocks = neurons // BLK
+    n = sum(sizes)
+    where = [(part, place) for part, size in enumerate(sizes) for place in range(size)]
     total = n * pixels
 
     def tile(block):
@@ -227,12 +241,14 @@
                 fresh[rows, :] = both[:, :BLK] + both[:, BLK:]
         for s in range(n):
             rows = slice(s * pixels, (s + 1) * pixels)
-            value = source[rows, lower:upper]
+            part, place = where[s]
+            value = source[part][place * pixels : (place + 1) * pixels, lower:upper]
             if has_ahead:
                 value = value - ahead[block % 2, rows, :]
             if previous is not None:
                 value = value - fresh[rows, :]
-            value = keep[s : s + 1, lower:upper] * jnp.maximum(value, 0.0)
+            kept = keeps[part][8 * place : 8 * place + 1, lower:upper]
+            value = kept * jnp.maximum(value, 0.0)
             fresh[rows, :] = value
             squares += jnp.sum((value * value).reshape(pixels // 8, 8, BLK), axis=0)
         if next_block is not None:
@@ -252,16 +268,16 @@
     for block in range(blocks):
         previous = block - 1 if block else None
         if block < last:
-            step(block, previous, block > 1, first, block + 1, [(0, block)])
+            step(block, previous, block > 1, firsts, block + 1, [(0, block)])
         else:
-            step(block, previous, block > 1, first, 0, [(0, last)])
+            step(block, previous, block > 1, firsts, 0, [(0, last)])
 
     @pl.loop(0, SWEEPS - 1)
     def _(_):
         for block in range(blocks):
             after = (block + 1) % blocks
             spans = [(0, block), (block + 1, blocks)]
-            step(block, (block - 1) % blocks, True, right, after, spans)
+            step(block, (block - 1) % blocks, True, rights, after, spans)
 
     out_ref[...] = join3(dot(jnp.concatenate(split3(result[...]), axis=0), perm[...]))
 
@@ -389,42 +405,61 @@
         *[y[k] for k in range(1, m)],
         *[blob for _, blob in blobs],
     )
-    got = {0: mine}
+
+    def unpack(group):
+        args, halves = [column], []
+        for s in group:
+            args += [got[s], others[s]] if s else [own, members, g]
+            halves.append(s == 0)
+        size = len(group) * pixels
+        outs = (
+            shape((size, neurons), f32),
+            shape((size, neurons), f32),
+            shape((8 * len(group), neurons), f32),
+        )
+        if 0 in group:
+            outs += (shape((2 * neurons, 2 * neurons), bf16),)
+        flops = 14 * size * width * neurons
+        scratch = [((neurons, width), bf16), ((pixels, 2 * width), f32)]
+        kernel = functools.partial(unpack_kernel, halves, len(args) - 1)
+        return call(kernel, flops, outs, scratch, UNPACK_MIB, *args)
+
+    got, others, groups = {0: mine}, {}, []
     for bit in bits:
         got[bit] = swap(mine, bit, 0)
     got[1] = swap(mine, 1, 0)
-    others = {}
     for bit in bits[::-1]:
         got[bit ^ 1] = swap(got[bit], 1, 0)
         if bit != bits[0]:
             for s in [s for s in list(got) if s & -s > bit]:
                 got[s ^ bit] = swap(got[s], bit, 0)
-    for s in list(got):
-        if s and s ^ 1 not in got:
-            got[s ^ 1] = swap(got[s], 1, 0)
-    for s in got:
-        if s:
-            others[s] = swap(got[s], 0, 1)
-    mines = [got[s] for s in range(1, n)]
-    others = [others[s] for s in range(1, n)]
+    early = [1, bits[-1]] if bits else [1]
+    for s in early:
+        others[s] = swap(got[s], 0, 1)
+    missing = [s ^ 1 for s in got if s ^ 1 not in got]
+    for s in missing:
+        got[s] = swap(got[s ^ 1], 1, 0)
+    rest = [s for s in got if s and s not in others]
+    for s in rest:
+        others[s] = swap(got[s], 0, 1)
+    groups = [[0], early, [s for s in got if s and s not in early]]
+    groups = [group for group in groups if group]
+    parts = [unpack(group) for group in groups]
     return call(
-        functools.partial(sweep_kernel, n),
+        functools.partial(sweep_kernel, [len(group) for group in groups]),
         2 * SWEEPS * 4 * total * neurons * neurons,
         shape((pixels, neurons), f32),
         [
-            ((neurons, width), bf16),
-            ((pixels, 2 * width), f32),
-            ((n, neurons), f32),
-            ((total, neurons), f32),
-            ((total, neurons), f32),
-            ((2 * neurons, 2 * neurons), bf16),
             ((total, 2 * neurons), bf16),
             ((2, total, BLK), f32),
             ((total, BLK), f32),
             ((pixels, neurons), f32),
         ],
-        40,
-        column, perm, members, own, g, *mines, *others,
+        SWEEP_MIB,
+        perm, parts[0][3],
+        *[part[0] for part in parts],
+        *[part[1] for part in parts],
+        *[part[2] for part in parts],
     )
 
 

time: 121 us -> 116 us (0.959)
  waiting for transfers between devices: 42.3 us -> 35.4 us
    ppermute x41, waiting for transfers between devices: 42.3 us -> 35.4 us  [swap(): return lax.ppermute(x, ('pix', 'frm'), pairs)]
    pallas_call x3 -> x6, Pallas kernels: 46.6 us -> 47.2 us  [call(): pl.pallas_call(kernel, out_shape=outs, in_specs=[vmem] * len(args), out_s...]
  transfers between devices with their start and end apart: 41 -> 41, of which waited for: 15 -> 15; matrix products, arithmetic and copies ran while one was open for 0% -> 0% of each run, Pallas kernels for 1% -> 3%
where the time goes in v1:
time: 116 us; the launch traced here: 115 us
  Pallas kernels  47.2 us (41%)
  waiting for transfers between devices  35.4 us (31%)
  starting transfers between devices  28.3 us (24%)
  local copies, waits for them, and re-layouts  4.24 us (4%)
    pallas_call x6, Pallas kernels, call(): pl.pallas_call(kernel, out_shape=outs, in_specs=[vmem] * len(args), out_s...  47.2 us
    ppermute x41, waiting for transfers between devices, swap(): return lax.ppermute(x, ('pix', 'frm'), pairs)  35.4 us
    ppermute x41, starting transfers between devices, swap(): return lax.ppermute(x, ('pix', 'frm'), pairs)  28.3 us
    unnamed x11, local copies, waits for them, and re-layouts  4.22 us
  transfers between devices with their start and end apart: 41, of which 15 were waited for; matrix products, arithmetic and copies ran while one was open for 0% of the time, Pallas kernels for 3%

profile of v1, /device:TPU:0, one launch (start us, length us, event | category | flops | bytes accessed | tf_op | source)
XLA Modules:
  0.0 115.4 jit_solution(16147818878895307694)
XLA Ops:
  0.0 4.1 %collective-permute-start.4 = (bf16[128,512]{1,0:T(8,128)(2,1)}, bf16[128,512]{1,0:T(8,128)(2,1)S(1)}, u32[]{:S(2)}, u32[]{:S(2)}) collective-permute-start(bf16[128,512]{1,0:T(8,128)(2,1)} %traces_ref.1), channel_id=1, source_target_pairs={{0,16},{1,17},{2,18},{3,19},{4,20},{5,21},{6,22},{7,23},{8,24},{9,... | collective-permute-start | bytes 393224 | tf_op jit(solution)/shard_map/ppermute | solution.py:293
  4.1 1.5 %collective-permute-start.1 = (bf16[128,512]{1,0:T(8,128)(2,1)}, bf16[128,512]{1,0:T(8,128)(2,1)S(1)}, u32[]{:S(2)}, u32[]{:S(2)}) collective-permute-start(bf16[128,512]{1,0:T(8,128)(2,1)} %frames_ref.1), channel_id=1, source_target_pairs={{0,2},{1,3},{2,0},{3,1},{4,6},{5,7},{6,4},{7,5},{8,10},{9,11},{10,... | collective-permute-start | bytes 393224 | tf_op jit(solution)/shard_map/ppermute | solution.py:293
  5.6 1.6 %collective-permute-start.5 = (bf16[128,512]{1,0:T(8,128)(2,1)}, bf16[128,512]{1,0:T(8,128)(2,1)S(1)}, u32[]{:S(2)}, u32[]{:S(2)}) collective-permute-start(bf16[128,512]{1,0:T(8,128)(2,1)} %traces_ref.1), channel_id=1, source_target_pairs={{0,8},{1,9},{2,10},{3,11},{4,12},{5,13},{6,14},{7,15},{8,0},{9,1},... | collective-permute-start | bytes 393224 | tf_op jit(solution)/shard_map/ppermute | solution.py:293
  7.2 0.5 collective-permute-start.3
  7.7 3.0 %collective-permute-done.4 = bf16[128,512]{1,0:T(8,128)(2,1)S(1)} collective-permute-done((bf16[128,512]{1,0:T(8,128)(2,1)}, bf16[128,512]{1,0:T(8,128)(2,1)S(1)}, u32[]{:S(2)}, u32[]{:S(2)}) %collective-permute-start.4) | collective-permute-done | bytes 131104 | tf_op jit(solution)/shard_map/ppermute | solution.py:293
  10.7 1.5 %collective-permute-start.9 = (bf16[128,512]{1,0:T(8,128)(2,1)}, bf16[128,512]{1,0:T(8,128)(2,1)S(1)}, u32[]{:S(2)}, u32[]{:S(2)}) collective-permute-start(bf16[128,512]{1,0:T(8,128)(2,1)} %traces_ref.1), channel_id=1, source_target_pairs={{0,4},{1,5},{2,6},{3,7},{4,0},{5,1},{6,2},{7,3},{8,12},{9,13},{10,... | collective-permute-start | bytes 393224 | tf_op jit(solution)/shard_map/ppermute | solution.py:293
  12.2 1.6 %collective-permute-start.11 = (bf16[128,512]{1,0:T(8,128)(2,1)}, bf16[128,512]{1,0:T(8,128)(2,1)S(1)}, u32[]{:S(2)}, u32[]{:S(2)}) collective-permute-start(bf16[128,512]{1,0:T(8,128)(2,1)} %traces_ref.1), channel_id=1, source_target_pairs={{0,2},{1,3},{2,0},{3,1},{4,6},{5,7},{6,4},{7,5},{8,10},{9,11},{10,... | collective-permute-start | bytes 393224 | tf_op jit(solution)/shard_map/ppermute | solution.py:293
  13.9 0.0 collective-permute-done.refs_1_
  13.9 0.6 collective-permute-start.17
  14.4 0.7 collective-permute-start.7
  15.2 0.7 collective-permute-done.9.refs_19_
  15.9 2.2 %collective-permute-done.11.refs_20_ = bf16[128,512]{1,0:T(8,128)(2,1)S(1)} collective-permute-done((bf16[128,512]{1,0:T(8,128)(2,1)}, bf16[128,512]{1,0:T(8,128)(2,1)S(1)}, u32[]{:S(2)}, u32[]{:S(2)}) %collective-permute-start.11) | collective-permute-done | bytes 131104 | tf_op jit(solution)/shard_map/ppermute | solution.py:293
  18.0 0.0 collective-permute-start.6
  18.0 0.5 collective-permute-start.12
  18.5 1.5 %collective-permute-done.7.refs_8_ = bf16[128,512]{1,0:T(8,128)(2,1)S(1)} collective-permute-done((bf16[128,512]{1,0:T(8,128)(2,1)S(1)}, bf16[128,512]{1,0:T(8,128)(2,1)S(1)}, u32[]{:S(2)}, u32[]{:S(2)}) %collective-permute-start.7) | collective-permute-done | bytes 131104 | tf_op jit(solution)/shard_map/ppermute | solution.py:293
  20.1 1.5 %collective-permute-start.13 = (bf16[128,512]{1,0:T(8,128)(2,1)S(1)}, bf16[128,512]{1,0:T(8,128)(2,1)S(1)}, u32[]{:S(2)}, u32[]{:S(2)}) collective-permute-start(bf16[128,512]{1,0:T(8,128)(2,1)S(1)} %collective-permute-done.9.refs_19_), channel_id=1, source_target_pairs={{0,2},{1,3},{2,0},{3,1},{4,6},{5,7},{6,4},{7,5},{8,10},{9,11},{10,... | collective-permute-start | bytes 393224 | tf_op jit(solution)/shard_map/ppermute | solution.py:293
  21.6 0.0 collective-permute-done.10.refs_9_
  21.6 0.5 collective-permute-start.15
  22.1 0.0 collective-permute-start.8
  22.1 1.4 %collective-permute-done.17.refs_23_ = bf16[256,512]{1,0:T(8,128)(2,1)S(1)} collective-permute-done((bf16[256,512]{1,0:T(8,128)(2,1)S(1)}, bf16[256,512]{1,0:T(8,128)(2,1)S(1)}, u32[]{:S(2)}, u32[]{:S(2)}) %collective-permute-start.17) | collective-permute-done | bytes 262176 | tf_op jit(solution)/shard_map/ppermute | solution.py:293
  23.6 0.4 collective-permute-start.19
  24.0 1.9 %collective-permute-done.13.refs_21_ = bf16[128,512]{1,0:T(8,128)(2,1)S(1)} collective-permute-done((bf16[128,512]{1,0:T(8,128)(2,1)S(1)}, bf16[128,512]{1,0:T(8,128)(2,1)S(1)}, u32[]{:S(2)}, u32[]{:S(2)}) %collective-permute-start.13) | collective-permute-done | bytes 131104 | tf_op jit(solution)/shard_map/ppermute | solution.py:293
  25.9 0.0 collective-permute-start.14
  25.9 0.0 collective-permute-done.6.refs_5_
  25.9 0.5 collective-permute-start.21
  26.4 0.0 collective-permute-done.8.refs_7_
  26.4 1.4 %collective-permute-start.23 = (bf16[128,512]{1,0:T(8,128)(2,1)S(1)}, bf16[128,512]{1,0:T(8,128)(2,1)S(1)}, u32[]{:S(2)}, u32[]{:S(2)}) collective-permute-start(bf16[128,512]{1,0:T(8,128)(2,1)S(1)} %collective-permute-done.7.refs_8_), channel_id=1, source_target_pairs={{0,2},{1,3},{2,0},{3,1},{4,6},{5,7},{6,4},{7,5},{8,10},{9,11},{10,... | collective-permute-start | bytes 393224 | tf_op jit(solution)/shard_map/ppermute | solution.py:293
  27.9 0.0 collective-permute-done.14.refs_11_
  27.9 1.6 %collective-permute-start.25 = (bf16[128,512]{1,0:T(8,128)(2,1)S(1)}, bf16[128,512]{1,0:T(8,128)(2,1)S(1)}, u32[]{:S(2)}, u32[]{:S(2)}) collective-permute-start(bf16[128,512]{1,0:T(8,128)(2,1)S(1)} %collective-permute-done.7.refs_8_), channel_id=1, source_target_pairs={{0,6},{1,7},{2,4},{3,5},{4,2},{5,3},{6,0},{7,1},{8,14},{9,15},{10,... | collective-permute-start | bytes 393224 | tf_op jit(solution)/shard_map/ppermute | solution.py:293
  29.4 1.3 %collective-permute-done.15.refs_22_ = bf16[256,512]{1,0:T(8,128)(2,1)S(1)} collective-permute-done((bf16[256,512]{1,0:T(8,128)(2,1)S(1)}, bf16[256,512]{1,0:T(8,128)(2,1)S(1)}, u32[]{:S(2)}, u32[]{:S(2)}) %collective-permute-start.15) | collective-permute-done | bytes 262176 | tf_op jit(solution)/shard_map/ppermute | solution.py:293
  30.8 0.0 collective-permute-start.18
  30.8 8.0 %collective-permute-done.21.refs_25_ = bf16[128,512]{1,0:T(8,128)(2,1)S(1)} collective-permute-done((bf16[128,512]{1,0:T(8,128)(2,1)S(1)}, bf16[128,512]{1,0:T(8,128)(2,1)S(1)}, u32[]{:S(2)}, u32[]{:S(2)}) %collective-permute-start.21) | collective-permute-done | bytes 131104 | tf_op jit(solution)/shard_map/ppermute | solution.py:293
  38.8 0.0 collective-permute-start.22
  38.8 0.5 collective-permute-start.16
  39.3 0.1 collective-permute-start.20
  39.4 0.7 collective-permute-done.25.refs_27_
  40.1 0.0 collective-permute-done.22.refs_15_
  40.1 0.5 collective-permute-start.26
  40.6 1.0 copy-done
  41.6 0.9 copy-done.1
  42.5 0.9 copy-done.2
  43.4 0.7 copy-done.3
  44.1 0.7 copy-done.4
  44.8 1.5 %shard_map.55 = (s32[1024,128]{1,0:T(8,128)S(1)}, bf16[1024,1024]{1,0:T(8,128)(2,1)S(1)}, bf16[1024,256]{1,0:T(8,128)(2,1)S(1)}, bf16[256,1024]{1,0:T(8,128)(2,1...) custom-call(s32[1,1024]{1,0:T(1,128)S(1)} %bitcast.1, ...), custom_call_target="tpu_custom_call" | custom-call | flops 805306368 | bytes 795648 | tf_op jit(solution)/shard_map/pallas_call | solution.py:304
  46.3 12.7 %shard_map.56 = (bf16[1024,2048]{1,0:T(8,128)(2,1)S(1)}, f32[128,512]{1,0:T(8,128)S(1)}, f32[72,512]{1,0:T(8,128)S(1)}) custom-call(bf16[1024,1024]{1,0:T(8,128)(2,1)S(1)} %get-tuple-element.25.perm, bf16[1024,256]{1,0:T(8,128)(2,1)S(1)} %get-tuple-element.27.members.refs_2_, bf16[256,1024]{1,0:T(8,128)(2,1)S(1)} %get-tuple-element.28.foot_hl, ...), custom_call_target="tpu_custom_call" | custom-call | flops 8589934592 | bytes 7880704 | tf_op jit(solution)/shard_map/pallas_call | solution.py:304
  59.1 2.7 %collective-permute-start.31 = (f32[72,512]{1,0:T(8,128)S(1)}, f32[72,512]{1,0:T(8,128)S(1)}, u32[]{:S(2)}, u32[]{:S(2)}) collective-permute-start(f32[72,512]{1,0:T(8,128)S(1)} %get-tuple-element.36), channel_id=1, source_target_pairs={{0,16},{1,17},{2,18},{3,19},{4,20},{5,21},{6,22},{7,23},{8,24},{9,... | collective-permute-start | bytes 442376 | tf_op jit(solution)/shard_map/ppermute | solution.py:293
  61.7 0.5 collective-permute-start.27
  62.2 1.5 %collective-permute-start.29 = (f32[72,512]{1,0:T(8,128)S(1)}, f32[72,512]{1,0:T(8,128)S(1)}, u32[]{:S(2)}, u32[]{:S(2)}) collective-permute-start(f32[72,512]{1,0:T(8,128)S(1)} %get-tuple-element.36), channel_id=1, source_target_pairs={{0,8},{1,9},{2,10},{3,11},{4,12},{5,13},{6,14},{7,15},{8,0},{9,1},... | collective-permute-start | bytes 442376 | tf_op jit(solution)/shard_map/ppermute | solution.py:293
  63.7 5.4 %collective-permute-done.31.refs_1_ = f32[72,512]{1,0:T(8,128)S(1)} collective-permute-done((f32[72,512]{1,0:T(8,128)S(1)}, f32[72,512]{1,0:T(8,128)S(1)}, u32[]{:S(2)}, u32[]{:S(2)}) %collective-permute-start.31) | collective-permute-done | bytes 147488 | tf_op jit(solution)/shard_map/ppermute | solution.py:293
  69.1 0.5 collective-permute-start.35
  69.6 0.1 collective-permute-done.29.refs_3_
  69.7 0.4 collective-permute-start.30
  70.1 1.1 collective-permute-start.33
  71.2 1.0 collective-permute-start.37
  72.2 2.1 %collective-permute-done.35.refs_5_ = f32[72,512]{1,0:T(8,128)S(1)} collective-permute-done((f32[72,512]{1,0:T(8,128)S(1)}, f32[72,512]{1,0:T(8,128)S(1)}, u32[]{:S(2)}, u32[]{:S(2)}) %collective-permute-start.35) | collective-permute-done | bytes 147488 | tf_op jit(solution)/shard_map/ppermute | solution.py:293
  74.2 0.5 collective-permute-start.39
  74.8 0.5 collective-permute-start.36
  75.3 1.6 %collective-permute-done.33.refs_3_ = f32[72,512]{1,0:T(8,128)S(1)} collective-permute-done((f32[72,512]{1,0:T(8,128)S(1)}, f32[72,512]{1,0:T(8,128)S(1)}, u32[]{:S(2)}, u32[]{:S(2)}) %collective-permute-start.33) | collective-permute-done | bytes 147488 | tf_op jit(solution)/shard_map/ppermute | solution.py:293
  76.8 3.2 %collective-permute-done.37.refs_7_ = f32[72,512]{1,0:T(8,128)S(1)} collective-permute-done((f32[72,512]{1,0:T(8,128)S(1)}, f32[72,512]{1,0:T(8,128)S(1)}, u32[]{:S(2)}, u32[]{:S(2)}) %collective-permute-start.37) | collective-permute-done | bytes 147488 | tf_op jit(solution)/shard_map/ppermute | solution.py:293
  80.0 2.3 %collective-permute-done.39.refs_9_ = f32[72,512]{1,0:T(8,128)S(1)} collective-permute-done((f32[72,512]{1,0:T(8,128)S(1)}, f32[72,512]{1,0:T(8,128)S(1)}, u32[]{:S(2)}, u32[]{:S(2)}) %collective-permute-start.39) | collective-permute-done | bytes 147488 | tf_op jit(solution)/shard_map/ppermute | solution.py:293
  82.3 1.1 shard_map.57
  83.4 1.2 %shard_map.58 = (f32[256,1024]{1,0:T(8,128)S(1)}, f32[256,1024]{1,0:T(8,128)S(1)}, f32[16,1024]{1,0:T(8,128)S(1)}) custom-call(s32[1024,128]{1,0:T(8,128)S(1)} %get-tuple-element.26.refs_0_, f32[72,512]{1,0:T(8,128)S(1)} %collective-permute-done.27.refs_1_, f32[72,512]{1,0:T(8,128)S(1)} %collective-permute-done.28.refs_2_, ...), custom_call_target="tpu_custom_call" | custom-call | flops 939524096 | bytes 1114112 | tf_op jit(solution)/shard_map/pallas_call | solution.py:304
  84.7 2.8 %shard_map.59 = (f32[640,1024]{1,0:T(8,128)S(1)}, f32[640,1024]{1,0:T(8,128)S(1)}, f32[40,1024]{1,0:T(8,128)S(1)}) custom-call(s32[1024,128]{1,0:T(8,128)S(1)} %get-tuple-element.26.refs_0_, f32[72,512]{1,0:T(8,128)S(1)} %collective-permute-done.31.refs_1_, f32[72,512]{1,0:T(8,128)S(1)} %collective-permute-done.32.refs_2_, ...), custom_call_target="tpu_custom_call" | custom-call | flops 2348810240 | bytes 1998848 | tf_op jit(solution)/shard_map/pallas_call | solution.py:304
  87.5 27.9 %shard_map.60 = f32[128,1024]{1,0:T(8,128)} custom-call(bf16[1024,1024]{1,0:T(8,128)(2,1)S(1)} %get-tuple-element.25.perm, bf16[2048,2048]{1,0:T(8,128)(2,1)S(1)} %get-tuple-element.34.weights, f32[128,1024]{1,0:T(8,128)S(1)} %get-tuple-element.35.refs_0_, f32[256,1024]{1,0:T(8,128)S(1)} %get-tuple-element.37.refs_1_, ...), custom_call_target="tpu_custom_call" | custom-call | flops 25769803776 | bytes 19136512 | tf_op jit(solution)/shard_map/pallas_call | solution.py:304
  (37 shorter events, 0.1 us)
Async XLA Ops:
  0.0 10.7 %collective-permute-start.4 = (bf16[128,512]{1,0:T(8,128)(2,1)}, bf16[128,512]{1,0:T(8,128)(2,1)S(1)}, u32[]{:S(2)}, u32[]{:S(2)}) collective-permute-start(bf16[128,512]{1,0:T(8,128)(2,1)} %traces_ref.1), channel_id=1, source_target_pairs={{0,16},{1,17},{2,18},{3,19},{4,20},{5,21},{6,22},{7,23},{8,24},{9,... | collective-permute-start | bytes 393224 | tf_op jit(solution)/shard_map/ppermute | solution.py:293
  4.1 8.2 %collective-permute-start.1 = (bf16[128,512]{1,0:T(8,128)(2,1)}, bf16[128,512]{1,0:T(8,128)(2,1)S(1)}, u32[]{:S(2)}, u32[]{:S(2)}) collective-permute-start(bf16[128,512]{1,0:T(8,128)(2,1)} %frames_ref.1), channel_id=1, source_target_pairs={{0,2},{1,3},{2,0},{3,1},{4,6},{5,7},{6,4},{7,5},{8,10},{9,11},{10,... | collective-permute-start | bytes 393224 | tf_op jit(solution)/shard_map/ppermute | solution.py:293
  5.6 8.2 %collective-permute-start.5 = (bf16[128,512]{1,0:T(8,128)(2,1)}, bf16[128,512]{1,0:T(8,128)(2,1)S(1)}, u32[]{:S(2)}, u32[]{:S(2)}) collective-permute-start(bf16[128,512]{1,0:T(8,128)(2,1)} %traces_ref.1), channel_id=1, source_target_pairs={{0,8},{1,9},{2,10},{3,11},{4,12},{5,13},{6,14},{7,15},{8,0},{9,1},... | collective-permute-start | bytes 393224 | tf_op jit(solution)/shard_map/ppermute | solution.py:293
  7.2 6.7 %collective-permute-start = (bf16[128,512]{1,0:T(8,128)(2,1)}, bf16[128,512]{1,0:T(8,128)(2,1)S(1)}, u32[]{:S(2)}, u32[]{:S(2)}) collective-permute-start(bf16[128,512]{1,0:T(8,128)(2,1)} %frames_ref.1), channel_id=1, source_target_pairs={{0,1},{1,0},{2,3},{3,2},{4,5},{5,4},{6,7},{7,6},{8,9},{9,8},{10,11... | collective-permute-start | bytes 393224 | tf_op jit(solution)/shard_map/ppermute | solution.py:293
  7.2 7.3 %collective-permute-start.3 = (bf16[128,512]{1,0:T(8,128)(2,1)}, bf16[128,512]{1,0:T(8,128)(2,1)S(1)}, u32[]{:S(2)}, u32[]{:S(2)}) collective-permute-start(bf16[128,512]{1,0:T(8,128)(2,1)} %traces_ref.1), channel_id=1, source_target_pairs={{0,1},{1,0},{2,3},{3,2},{4,5},{5,4},{6,7},{7,6},{8,9},{9,8},{10,11... | collective-permute-start | bytes 393224 | tf_op jit(solution)/shard_map/ppermute | solution.py:293
  10.7 5.2 %collective-permute-start.9 = (bf16[128,512]{1,0:T(8,128)(2,1)}, bf16[128,512]{1,0:T(8,128)(2,1)S(1)}, u32[]{:S(2)}, u32[]{:S(2)}) collective-permute-start(bf16[128,512]{1,0:T(8,128)(2,1)} %traces_ref.1), channel_id=1, source_target_pairs={{0,4},{1,5},{2,6},{3,7},{4,0},{5,1},{6,2},{7,3},{8,12},{9,13},{10,... | collective-permute-start | bytes 393224 | tf_op jit(solution)/shard_map/ppermute | solution.py:293
  12.2 5.8 %collective-permute-start.11 = (bf16[128,512]{1,0:T(8,128)(2,1)}, bf16[128,512]{1,0:T(8,128)(2,1)S(1)}, u32[]{:S(2)}, u32[]{:S(2)}) collective-permute-start(bf16[128,512]{1,0:T(8,128)(2,1)} %traces_ref.1), channel_id=1, source_target_pairs={{0,2},{1,3},{2,0},{3,1},{4,6},{5,7},{6,4},{7,5},{8,10},{9,11},{10,... | collective-permute-start | bytes 393224 | tf_op jit(solution)/shard_map/ppermute | solution.py:293
  13.8 4.2 %collective-permute-start.2 = (bf16[128,512]{1,0:T(8,128)(2,1)S(1)}, bf16[128,512]{1,0:T(8,128)(2,1)S(1)}, u32[]{:S(2)}, u32[]{:S(2)}) collective-permute-start(bf16[128,512]{1,0:T(8,128)(2,1)S(1)} %collective-permute-done.1.refs_2_), channel_id=1, source_target_pairs={{0,1},{1,0},{2,3},{3,2},{4,5},{5,4},{6,7},{7,6},{8,9},{9,8},{10,11... | collective-permute-start | bytes 393224 | tf_op jit(solution)/shard_map/ppermute | solution.py:293
  13.9 9.7 %collective-permute-start.17 = (bf16[256,512]{1,0:T(8,128)(2,1)S(1)}, bf16[256,512]{1,0:T(8,128)(2,1)S(1)}, u32[]{:S(2)}, u32[]{:S(2)}) collective-permute-start(bf16[256,512]{1,0:T(8,128)(2,1)S(1)} %constant_dynamic-update-slice_fusion.refs_6_), channel_id=1, source_target_pairs={{0,2},{1,3},{2,0},{3,1},{4,6},{5,7},{6,4},{7,5},{8,10},{9,11},{10,... | collective-permute-start | bytes 786440 | tf_op jit(solution)/shard_map/ppermute | solution.py:293
  14.4 5.6 %collective-permute-start.7 = (bf16[128,512]{1,0:T(8,128)(2,1)S(1)}, bf16[128,512]{1,0:T(8,128)(2,1)S(1)}, u32[]{:S(2)}, u32[]{:S(2)}) collective-permute-start(bf16[128,512]{1,0:T(8,128)(2,1)S(1)} %collective-permute-done.4), channel_id=1, source_target_pairs={{0,8},{1,9},{2,10},{3,11},{4,12},{5,13},{6,14},{7,15},{8,0},{9,1},... | collective-permute-start | bytes 393224 | tf_op jit(solution)/shard_map/ppermute | solution.py:293
  15.9 5.7 %collective-permute-start.10 = (bf16[128,512]{1,0:T(8,128)(2,1)S(1)}, bf16[128,512]{1,0:T(8,128)(2,1)S(1)}, u32[]{:S(2)}, u32[]{:S(2)}) collective-permute-start(bf16[128,512]{1,0:T(8,128)(2,1)S(1)} %collective-permute-done.9.refs_19_), channel_id=1, source_target_pairs={{0,1},{1,0},{2,3},{3,2},{4,5},{5,4},{6,7},{7,6},{8,9},{9,8},{10,11... | collective-permute-start | bytes 393224 | tf_op jit(solution)/shard_map/ppermute | solution.py:293
  18.0 7.9 %collective-permute-start.6 = (bf16[256,512]{1,0:T(8,128)(2,1)S(1)}, bf16[256,512]{1,0:T(8,128)(2,1)S(1)}, u32[]{:S(2)}, u32[]{:S(2)}) collective-permute-start(bf16[256,512]{1,0:T(8,128)(2,1)S(1)} %constant_dynamic-update-slice_fusion.refs_6_), channel_id=1, source_target_pairs={{0,1},{1,0},{2,3},{3,2},{4,5},{5,4},{6,7},{7,6},{8,9},{9,8},{10,11... | collective-permute-start | bytes 786440 | tf_op jit(solution)/shard_map/ppermute | solution.py:293
  18.0 4.1 %collective-permute-start.12 = (bf16[128,512]{1,0:T(8,128)(2,1)S(1)}, bf16[128,512]{1,0:T(8,128)(2,1)S(1)}, u32[]{:S(2)}, u32[]{:S(2)}) collective-permute-start(bf16[128,512]{1,0:T(8,128)(2,1)S(1)} %collective-permute-done.11.refs_20_), channel_id=1, source_target_pairs={{0,1},{1,0},{2,3},{3,2},{4,5},{5,4},{6,7},{7,6},{8,9},{9,8},{10,11... | collective-permute-start | bytes 393224 | tf_op jit(solution)/shard_map/ppermute | solution.py:293
  20.1 5.8 %collective-permute-start.13 = (bf16[128,512]{1,0:T(8,128)(2,1)S(1)}, bf16[128,512]{1,0:T(8,128)(2,1)S(1)}, u32[]{:S(2)}, u32[]{:S(2)}) collective-permute-start(bf16[128,512]{1,0:T(8,128)(2,1)S(1)} %collective-permute-done.9.refs_19_), channel_id=1, source_target_pairs={{0,2},{1,3},{2,0},{3,1},{4,6},{5,7},{6,4},{7,5},{8,10},{9,11},{10,... | collective-permute-start | bytes 393224 | tf_op jit(solution)/shard_map/ppermute | solution.py:293
  21.6 9.2 %collective-permute-start.15 = (bf16[256,512]{1,0:T(8,128)(2,1)S(1)}, bf16[256,512]{1,0:T(8,128)(2,1)S(1)}, u32[]{:S(2)}, u32[]{:S(2)}) collective-permute-start(bf16[256,512]{1,0:T(8,128)(2,1)S(1)} %constant_dynamic-update-slice_fusion.refs_6_), channel_id=1, source_target_pairs={{0,4},{1,5},{2,6},{3,7},{4,0},{5,1},{6,2},{7,3},{8,12},{9,13},{10,... | collective-permute-start | bytes 786440 | tf_op jit(solution)/shard_map/ppermute | solution.py:293
  22.1 4.3 %collective-permute-start.8 = (bf16[128,512]{1,0:T(8,128)(2,1)S(1)}, bf16[128,512]{1,0:T(8,128)(2,1)S(1)}, u32[]{:S(2)}, u32[]{:S(2)}) collective-permute-start(bf16[128,512]{1,0:T(8,128)(2,1)S(1)} %collective-permute-done.7.refs_8_), channel_id=1, source_target_pairs={{0,1},{1,0},{2,3},{3,2},{4,5},{5,4},{6,7},{7,6},{8,9},{9,8},{10,11... | collective-permute-start | bytes 393224 | tf_op jit(solution)/shard_map/ppermute | solution.py:293
  23.6 15.7 %collective-permute-start.19 = (bf16[256,512]{1,0:T(8,128)(2,1)S(1)}, bf16[256,512]{1,0:T(8,128)(2,1)S(1)}, u32[]{:S(2)}, u32[]{:S(2)}) collective-permute-start(bf16[256,512]{1,0:T(8,128)(2,1)S(1)} %collective-permute-done.17.refs_23_), channel_id=1, source_target_pairs={{0,4},{1,5},{2,6},{3,7},{4,0},{5,1},{6,2},{7,3},{8,12},{9,13},{10,... | collective-permute-start | bytes 786440 | tf_op jit(solution)/shard_map/ppermute | solution.py:293
  25.9 1.9 %collective-permute-start.14 = (bf16[128,512]{1,0:T(8,128)(2,1)S(1)}, bf16[128,512]{1,0:T(8,128)(2,1)S(1)}, u32[]{:S(2)}, u32[]{:S(2)}) collective-permute-start(bf16[128,512]{1,0:T(8,128)(2,1)S(1)} %collective-permute-done.13.refs_21_), channel_id=1, source_target_pairs={{0,1},{1,0},{2,3},{3,2},{4,5},{5,4},{6,7},{7,6},{8,9},{9,8},{10,11... | collective-permute-start | bytes 393224 | tf_op jit(solution)/shard_map/ppermute | solution.py:293
  25.9 12.8 %collective-permute-start.21 = (bf16[128,512]{1,0:T(8,128)(2,1)S(1)}, bf16[128,512]{1,0:T(8,128)(2,1)S(1)}, u32[]{:S(2)}, u32[]{:S(2)}) collective-permute-start(bf16[128,512]{1,0:T(8,128)(2,1)S(1)} %collective-permute-done.7.refs_8_), channel_id=1, source_target_pairs={{0,4},{1,5},{2,6},{3,7},{4,0},{5,1},{6,2},{7,3},{8,12},{9,13},{10,... | collective-permute-start | bytes 393224 | tf_op jit(solution)/shard_map/ppermute | solution.py:293
  26.4 12.4 %collective-permute-start.23 = (bf16[128,512]{1,0:T(8,128)(2,1)S(1)}, bf16[128,512]{1,0:T(8,128)(2,1)S(1)}, u32[]{:S(2)}, u32[]{:S(2)}) collective-permute-start(bf16[128,512]{1,0:T(8,128)(2,1)S(1)} %collective-permute-done.7.refs_8_), channel_id=1, source_target_pairs={{0,2},{1,3},{2,0},{3,1},{4,6},{5,7},{6,4},{7,5},{8,10},{9,11},{10,... | collective-permute-start | bytes 393224 | tf_op jit(solution)/shard_map/ppermute | solution.py:293
  27.9 12.2 %collective-permute-start.25 = (bf16[128,512]{1,0:T(8,128)(2,1)S(1)}, bf16[128,512]{1,0:T(8,128)(2,1)S(1)}, u32[]{:S(2)}, u32[]{:S(2)}) collective-permute-start(bf16[128,512]{1,0:T(8,128)(2,1)S(1)} %collective-permute-done.7.refs_8_), channel_id=1, source_target_pairs={{0,6},{1,7},{2,4},{3,5},{4,2},{5,3},{6,0},{7,1},{8,14},{9,15},{10,... | collective-permute-start | bytes 393224 | tf_op jit(solution)/shard_map/ppermute | solution.py:293
  30.8 15.6 %collective-permute-start.18 = (bf16[256,512]{1,0:T(8,128)(2,1)S(1)}, bf16[256,512]{1,0:T(8,128)(2,1)S(1)}, u32[]{:S(2)}, u32[]{:S(2)}) collective-permute-start(bf16[256,512]{1,0:T(8,128)(2,1)S(1)} %collective-permute-done.17.refs_23_), channel_id=1, source_target_pairs={{0,1},{1,0},{2,3},{3,2},{4,5},{5,4},{6,7},{7,6},{8,9},{9,8},{10,11... | collective-permute-start | bytes 786440 | tf_op jit(solution)/shard_map/ppermute | solution.py:293
  38.8 1.3 %collective-permute-start.22 = (bf16[128,512]{1,0:T(8,128)(2,1)S(1)}, bf16[128,512]{1,0:T(8,128)(2,1)S(1)}, u32[]{:S(2)}, u32[]{:S(2)}) collective-permute-start(bf16[128,512]{1,0:T(8,128)(2,1)S(1)} %collective-permute-done.21.refs_25_), channel_id=1, source_target_pairs={{0,1},{1,0},{2,3},{3,2},{4,5},{5,4},{6,7},{7,6},{8,9},{9,8},{10,11... | collective-permute-start | bytes 393224 | tf_op jit(solution)/shard_map/ppermute | solution.py:293
  38.8 7.5 %collective-permute-start.16 = (bf16[256,512]{1,0:T(8,128)(2,1)S(1)}, bf16[256,512]{1,0:T(8,128)(2,1)S(1)}, u32[]{:S(2)}, u32[]{:S(2)}) collective-permute-start(bf16[256,512]{1,0:T(8,128)(2,1)S(1)} %collective-permute-done.15.refs_22_), channel_id=1, source_target_pairs={{0,1},{1,0},{2,3},{3,2},{4,5},{5,4},{6,7},{7,6},{8,9},{9,8},{10,11... | collective-permute-start | bytes 786440 | tf_op jit(solution)/shard_map/ppermute | solution.py:293
  39.3 7.1 %collective-permute-start.20 = (bf16[256,512]{1,0:T(8,128)(2,1)S(1)}, bf16[256,512]{1,0:T(8,128)(2,1)S(1)}, u32[]{:S(2)}, u32[]{:S(2)}) collective-permute-start(bf16[256,512]{1,0:T(8,128)(2,1)S(1)} %collective-permute-done.19.refs_24_), channel_id=1, source_target_pairs={{0,1},{1,0},{2,3},{3,2},{4,5},{5,4},{6,7},{7,6},{8,9},{9,8},{10,11... | collective-permute-start | bytes 786440 | tf_op jit(solution)/shard_map/ppermute | solution.py:293
  40.1 6.2 %collective-permute-start.24 = (bf16[128,512]{1,0:T(8,128)(2,1)S(1)}, bf16[128,512]{1,0:T(8,128)(2,1)S(1)}, u32[]{:S(2)}, u32[]{:S(2)}) collective-permute-start(bf16[128,512]{1,0:T(8,128)(2,1)S(1)} %collective-permute-done.23.refs_26_), channel_id=1, source_target_pairs={{0,1},{1,0},{2,3},{3,2},{4,5},{5,4},{6,7},{7,6},{8,9},{9,8},{10,11... | collective-permute-start | bytes 393224 | tf_op jit(solution)/shard_map/ppermute | solution.py:293
  40.1 6.2 %collective-permute-start.26 = (bf16[128,512]{1,0:T(8,128)(2,1)S(1)}, bf16[128,512]{1,0:T(8,128)(2,1)S(1)}, u32[]{:S(2)}, u32[]{:S(2)}) collective-permute-start(bf16[128,512]{1,0:T(8,128)(2,1)S(1)} %collective-permute-done.25.refs_27_), channel_id=1, source_target_pairs={{0,1},{1,0},{2,3},{3,2},{4,5},{5,4},{6,7},{7,6},{8,9},{9,8},{10,11... | collective-permute-start | bytes 393224 | tf_op jit(solution)/shard_map/ppermute | solution.py:293
  40.6 1.0 copy-start
  41.6 0.9 copy-start.1
  42.5 0.9 copy-start.2
  43.4 0.7 copy-start.3
  44.1 0.7 copy-start.4
  59.1 10.0 %collective-permute-start.31 = (f32[72,512]{1,0:T(8,128)S(1)}, f32[72,512]{1,0:T(8,128)S(1)}, u32[]{:S(2)}, u32[]{:S(2)}) collective-permute-start(f32[72,512]{1,0:T(8,128)S(1)} %get-tuple-element.36), channel_id=1, source_target_pairs={{0,16},{1,17},{2,18},{3,19},{4,20},{5,21},{6,22},{7,23},{8,24},{9,... | collective-permute-start | bytes 442376 | tf_op jit(solution)/shard_map/ppermute | solution.py:293
  61.7 7.9 %collective-permute-start.27 = (f32[72,512]{1,0:T(8,128)S(1)}, f32[72,512]{1,0:T(8,128)S(1)}, u32[]{:S(2)}, u32[]{:S(2)}) collective-permute-start(f32[72,512]{1,0:T(8,128)S(1)} %get-tuple-element.36), channel_id=1, source_target_pairs={{0,4},{1,5},{2,6},{3,7},{4,0},{5,1},{6,2},{7,3},{8,12},{9,13},{10,... | collective-permute-start | bytes 442376 | tf_op jit(solution)/shard_map/ppermute | solution.py:293
  62.2 7.5 %collective-permute-start.29 = (f32[72,512]{1,0:T(8,128)S(1)}, f32[72,512]{1,0:T(8,128)S(1)}, u32[]{:S(2)}, u32[]{:S(2)}) collective-permute-start(f32[72,512]{1,0:T(8,128)S(1)} %get-tuple-element.36), channel_id=1, source_target_pairs={{0,8},{1,9},{2,10},{3,11},{4,12},{5,13},{6,14},{7,15},{8,0},{9,1},... | collective-permute-start | bytes 442376 | tf_op jit(solution)/shard_map/ppermute | solution.py:293
  69.1 5.1 %collective-permute-start.35 = (f32[72,512]{1,0:T(8,128)S(1)}, f32[72,512]{1,0:T(8,128)S(1)}, u32[]{:S(2)}, u32[]{:S(2)}) collective-permute-start(f32[72,512]{1,0:T(8,128)S(1)} %collective-permute-done.31.refs_1_), channel_id=1, source_target_pairs={{0,8},{1,9},{2,10},{3,11},{4,12},{5,13},{6,14},{7,15},{8,0},{9,1},... | collective-permute-start | bytes 442376 | tf_op jit(solution)/shard_map/ppermute | solution.py:293
  69.6 5.1 %collective-permute-start.28 = (f32[72,512]{1,0:T(8,128)S(1)}, f32[72,512]{1,0:T(8,128)S(1)}, u32[]{:S(2)}, u32[]{:S(2)}) collective-permute-start(f32[72,512]{1,0:T(8,128)S(1)} %collective-permute-done.27.refs_1_), channel_id=1, source_target_pairs={{0,1},{1,0},{2,3},{3,2},{4,5},{5,4},{6,7},{7,6},{8,9},{9,8},{10,11... | collective-permute-start | bytes 442376 | tf_op jit(solution)/shard_map/ppermute | solution.py:293
  69.7 5.1 %collective-permute-start.30 = (f32[72,512]{1,0:T(8,128)S(1)}, f32[72,512]{1,0:T(8,128)S(1)}, u32[]{:S(2)}, u32[]{:S(2)}) collective-permute-start(f32[72,512]{1,0:T(8,128)S(1)} %collective-permute-done.29.refs_3_), channel_id=1, source_target_pairs={{0,1},{1,0},{2,3},{3,2},{4,5},{5,4},{6,7},{7,6},{8,9},{9,8},{10,11... | collective-permute-start | bytes 442376 | tf_op jit(solution)/shard_map/ppermute | solution.py:293
  70.1 6.7 %collective-permute-start.33 = (f32[72,512]{1,0:T(8,128)S(1)}, f32[72,512]{1,0:T(8,128)S(1)}, u32[]{:S(2)}, u32[]{:S(2)}) collective-permute-start(f32[72,512]{1,0:T(8,128)S(1)} %collective-permute-done.29.refs_3_), channel_id=1, source_target_pairs={{0,4},{1,5},{2,6},{3,7},{4,0},{5,1},{6,2},{7,3},{8,12},{9,13},{10,... | collective-permute-start | bytes 442376 | tf_op jit(solution)/shard_map/ppermute | solution.py:293
  71.2 8.8 %collective-permute-start.37 = (f32[72,512]{1,0:T(8,128)S(1)}, f32[72,512]{1,0:T(8,128)S(1)}, u32[]{:S(2)}, u32[]{:S(2)}) collective-permute-start(f32[72,512]{1,0:T(8,128)S(1)} %collective-permute-done.31.refs_1_), channel_id=1, source_target_pairs={{0,4},{1,5},{2,6},{3,7},{4,0},{5,1},{6,2},{7,3},{8,12},{9,13},{10,... | collective-permute-start | bytes 442376 | tf_op jit(solution)/shard_map/ppermute | solution.py:293
  74.2 8.1 %collective-permute-start.39 = (f32[72,512]{1,0:T(8,128)S(1)}, f32[72,512]{1,0:T(8,128)S(1)}, u32[]{:S(2)}, u32[]{:S(2)}) collective-permute-start(f32[72,512]{1,0:T(8,128)S(1)} %collective-permute-done.35.refs_5_), channel_id=1, source_target_pairs={{0,4},{1,5},{2,6},{3,7},{4,0},{5,1},{6,2},{7,3},{8,12},{9,13},{10,... | collective-permute-start | bytes 442376 | tf_op jit(solution)/shard_map/ppermute | solution.py:293
  74.7 9.9 %collective-permute-start.32 = (f32[72,512]{1,0:T(8,128)S(1)}, f32[72,512]{1,0:T(8,128)S(1)}, u32[]{:S(2)}, u32[]{:S(2)}) collective-permute-start(f32[72,512]{1,0:T(8,128)S(1)} %collective-permute-done.31.refs_1_), channel_id=1, source_target_pairs={{0,1},{1,0},{2,3},{3,2},{4,5},{5,4},{6,7},{7,6},{8,9},{9,8},{10,11... | collective-permute-start | bytes 442376 | tf_op jit(solution)/shard_map/ppermute | solution.py:293
  74.8 9.9 %collective-permute-start.36 = (f32[72,512]{1,0:T(8,128)S(1)}, f32[72,512]{1,0:T(8,128)S(1)}, u32[]{:S(2)}, u32[]{:S(2)}) collective-permute-start(f32[72,512]{1,0:T(8,128)S(1)} %collective-permute-done.35.refs_5_), channel_id=1, source_target_pairs={{0,1},{1,0},{2,3},{3,2},{4,5},{5,4},{6,7},{7,6},{8,9},{9,8},{10,11... | collective-permute-start | bytes 442376 | tf_op jit(solution)/shard_map/ppermute | solution.py:293
  76.8 7.8 %collective-permute-start.34 = (f32[72,512]{1,0:T(8,128)S(1)}, f32[72,512]{1,0:T(8,128)S(1)}, u32[]{:S(2)}, u32[]{:S(2)}) collective-permute-start(f32[72,512]{1,0:T(8,128)S(1)} %collective-permute-done.33.refs_3_), channel_id=1, source_target_pairs={{0,1},{1,0},{2,3},{3,2},{4,5},{5,4},{6,7},{7,6},{8,9},{9,8},{10,11... | collective-permute-start | bytes 442376 | tf_op jit(solution)/shard_map/ppermute | solution.py:293
  80.0 4.7 %collective-permute-start.38 = (f32[72,512]{1,0:T(8,128)S(1)}, f32[72,512]{1,0:T(8,128)S(1)}, u32[]{:S(2)}, u32[]{:S(2)}) collective-permute-start(f32[72,512]{1,0:T(8,128)S(1)} %collective-permute-done.37.refs_7_), channel_id=1, source_target_pairs={{0,1},{1,0},{2,3},{3,2},{4,5},{5,4},{6,7},{7,6},{8,9},{9,8},{10,11... | collective-permute-start | bytes 442376 | tf_op jit(solution)/shard_map/ppermute | solution.py:293
  82.3 2.4 %collective-permute-start.40 = (f32[72,512]{1,0:T(8,128)S(1)}, f32[72,512]{1,0:T(8,128)S(1)}, u32[]{:S(2)}, u32[]{:S(2)}) collective-permute-start(f32[72,512]{1,0:T(8,128)S(1)} %collective-permute-done.39.refs_9_), channel_id=1, source_target_pairs={{0,1},{1,0},{2,3},{3,2},{4,5},{5,4},{6,7},{7,6},{8,9},{9,8},{10,11... | collective-permute-start | bytes 442376 | tf_op jit(solution)/shard_map/ppermute | solution.py:293
